TPU v7x, 32 devices: a whole 2x2x4 slice. The times are simulated.
32 devices in a mesh: dp: 2 (over core), expert: 4 (over z), head: 4 (over y, x).
Axes of the slice: x: 2, y: 2, z: 4, core: 2. Of those that a mesh axis runs over, the one named last changes fastest.
Arguments:
- inputs: bfloat16 [4096, 1024], P(('dp', 'expert', 'head')), may hold values from -6 to 6
- cotangent: bfloat16 [4096, 1024], P(('dp', 'expert', 'head')), may hold values from -6 to 6
- segment_starts: int32 [4, 2], P('expert'), may hold values from 0 to 768, as said below
- routes: int32 [2, 4096, 8], P(None, ('dp', 'expert', 'head')), may hold values from 0 to 31, all different within a row; in each aligned block of 128 rows (0 to 127, 128 to 255, ..., all dimensions but the last counted through in order) at most 34 rows name the same one
- attention_gain: float32 [2, 1024], replicated, may hold values from 0.1 to 1.9
- mixture_gain: float32 [2, 1024], replicated, may hold values from 0.1 to 1.9
- query_weight: bfloat16 [2, 1024, 1024], P(None, 'expert', 'head'), may hold values from -0.1875 to 0.1875
- key_weight: bfloat16 [2, 1024, 512], P(None, 'expert', 'head'), may hold values from -0.1875 to 0.1875
- value_weight: bfloat16 [2, 1024, 512], P(None, 'expert', 'head'), may hold values from -0.1875 to 0.1875
- output_weight: bfloat16 [2, 1024, 1024], P(None, 'head', 'expert'), may hold values from -3 to 3
- router_weight: bfloat16 [2, 1024, 32], replicated, may hold values from -0.09375 to 0.09375
- expert_in: bfloat16 [2, 32, 1024, 1024], P(None, 'expert'), may hold values from -0.1875 to 0.1875
- expert_out: bfloat16 [2, 32, 512, 1024], P(None, 'expert'), may hold values from -0.75 to 0.75
Outputs:
- outputs: bfloat16 [4096, 1024], P(('dp', 'expert', 'head'))
- input_grad: float32 [4096, 1024], P(('dp', 'expert', 'head'))
- attention_gain_grad: float32 [2, 1024], replicated
- mixture_gain_grad: float32 [2, 1024], replicated
- query_grad: float32 [2, 1024, 1024], P(None, ('dp', 'expert'), 'head')
- key_grad: float32 [2, 1024, 512], P(None, ('dp', 'expert'), 'head')
- value_grad: float32 [2, 1024, 512], P(None, ('dp', 'expert'), 'head')
- output_grad: float32 [2, 1024, 1024], P(None, 'head', ('dp', 'expert'))
- router_grad: float32 [2, 1024, 32], replicated
- expert_in_grad: float32 [2, 32, 1024, 1024], P(None, 'expert', ('dp', 'head'))
- expert_out_grad: float32 [2, 32, 512, 1024], P(None, 'expert', ('dp', 'head'))
Inputs may be any that keep to these rules, and one draw needn't show every extreme that they name: `routes`: each row names 8 different experts. Within each aligned block of 128 rows in one layer, no expert is named by more than 34 rows, a bound that some block reaches. `segment_starts`: A sequence's 2 segments of 256 positions lie inside it, disjoint and in rising order, the s-th within the s-th of 2 equal parts of the sequence. A start of 0 and a start of 768 occur in every draw.
All inputs are finite; a program needn't handle non-finite values.
Results may differ from a plain program's by a relative error of at most 0.03.
Values may be sent and summed in bfloat16 or wider, within the bound.
A program may use at most 320 MiB of HBM per device.

v0:
```python
import jax
import jax.numpy as jnp
from jax import lax
from jax.sharding import PartitionSpec as P

HEAD_DIM = 64
BIDI = 256
CAP = 34


EPS = 1e-06
THETA = 10000.0
NEG = -1e30
HIGH = lax.Precision.HIGHEST


def split_up(x, dim, devices):
    before, after = (x.shape[:dim], x.shape[dim + 1 :])
    return jnp.moveaxis(x.reshape(*before, devices, -1, *after), dim, 0)


def sum_at_owner(x, axis, dim):
    pieces = split_up(x, dim, lax.axis_size(axis))
    arrived = lax.all_to_all(pieces, axis, split_axis=0, concat_axis=0, tiled=True)
    return arrived.astype(jnp.float32).sum(axis=0)


def side_by_side(arrays, axis, dim, along):
    widths = [a.shape[along] for a in arrays]
    both = jnp.concatenate(arrays, axis=along)
    whole = sum_at_owner(both, axis, dim)
    return tuple(jnp.split(whole, [sum(widths[:k]) for k in range(1, len(widths))], axis=along))


def rms_scale(values):
    return lax.rsqrt(jnp.mean(values * values, axis=-1, keepdims=True) + EPS)


def norm_back(values, factor, gain, grad):
    normed = values * factor
    gain_grad = jnp.sum(grad * normed, axis=0)
    inner = grad * gain
    return (factor * (inner - normed * jnp.mean(inner * normed, axis=-1, keepdims=True)), gain_grad)


def rope_tables(places, head_dim):
    half = head_dim // 2
    inverse = THETA ** (-(jnp.arange(half, dtype=jnp.float32) * 2.0 / head_dim))
    angle = places.astype(jnp.float32)[:, None] * inverse[None, :]
    angle = jnp.concatenate([angle, angle], axis=1)
    return (jnp.cos(angle)[:, None, :], jnp.sin(angle)[:, None, :])


def rotate(values, cosine, sine, sign):
    half = values.shape[-1] // 2
    turned = jnp.concatenate([-values[..., half:], values[..., :half]], axis=-1)
    return values * cosine + sign * turned * sine


def visible(query_pos, key_pos, starts):
    causal = key_pos[None, :] <= query_pos[:, None]
    query_in = (query_pos[:, None] >= starts[None, :]) & (
        query_pos[:, None] < starts[None, :] + BIDI
    )
    key_in = (key_pos[:, None] >= starts[None, :]) & (key_pos[:, None] < starts[None, :] + BIDI)
    shared = jnp.any(query_in[:, None, :] & key_in[None, :, :], axis=-1)
    return causal | shared


def slot_tables(hits, capacity):
    picks_flat = jnp.argmax(hits, axis=1)
    before = jnp.cumsum(hits, axis=0) - hits
    slot = jnp.sum(before * hits, axis=1)
    slot_of = picks_flat * capacity + slot
    total = hits.shape[0]
    owner_of = (
        jnp.full((hits.shape[1] * capacity,), total, jnp.int32)
        .at[slot_of]
        .set(jnp.arange(total, dtype=jnp.int32))
    )
    return (slot_of, owner_of)


def contract_rows(left, right):
    return lax.dot_general(
        left, right, (((0,), (0,)), ((), ())), preferred_element_type=jnp.float32
    )


def contract_cols(left, right):
    return lax.dot_general(
        left, right, (((1,), (1,)), ((), ())), preferred_element_type=jnp.float32
    )


def per_device(
    inputs,
    cotangent,
    segment_starts,
    routes,
    attention_gain,
    mixture_gain,
    query_weight,
    key_weight,
    value_weight,
    output_weight,
    router_weight,
    expert_in,
    expert_out,
):
    rows, width = inputs.shape
    half_len = rows * lax.axis_size("head")
    length = half_len * lax.axis_size("dp")
    block = min(512, half_len)
    nblocks = half_len // block
    head_dim = HEAD_DIM
    q_heads = query_weight.shape[2] // head_dim
    kv_heads = key_weight.shape[2] // head_dim
    share = q_heads // kv_heads
    layers = query_weight.shape[0]
    local_experts = expert_in.shape[1]
    owners = lax.axis_size("expert")
    all_experts = local_experts * owners
    capacity = CAP
    top = routes.shape[2]
    hidden_width = expert_out.shape[2]
    count = rows * top
    factor = head_dim ** (-0.5)
    offset = lax.axis_index("dp") * half_len
    positions = jnp.arange(length, dtype=jnp.int32)
    cosine, sine = rope_tables(positions, head_dim)
    cos_own = lax.dynamic_slice_in_dim(cosine, offset, half_len, 0)
    sin_own = lax.dynamic_slice_in_dim(sine, offset, half_len, 0)
    starts = segment_starts[0]
    block_ids = jnp.arange(nblocks, dtype=jnp.int32)
    expert_ids = jnp.arange(all_experts, dtype=jnp.int32)

    def block_scores(q_block, keys, index):
        query_pos = offset + index * block + jnp.arange(block, dtype=jnp.int32)
        mask = visible(query_pos, positions, starts)
        raw = (
            jnp.einsum("qcgd,kcd->cgqk", q_block, keys, preferred_element_type=jnp.float32) * factor
        )
        return jnp.where(mask[None, None], raw, NEG)

    current = inputs.astype(jnp.float32)
    saved = []
    for layer in range(layers):
        scale_one = rms_scale(current)
        normed_one = (current * scale_one * attention_gain[layer]).astype(jnp.bfloat16)
        full_rows = lax.all_gather(normed_one, ("dp", "head"), axis=0, tiled=True)
        own_rows = lax.dynamic_slice_in_dim(full_rows, offset, half_len, 0)
        weight_q, weight_k, weight_v, weight_o = (
            lax.all_gather(query_weight[layer], "expert", axis=0, tiled=True),
            lax.all_gather(key_weight[layer], "expert", axis=0, tiled=True),
            lax.all_gather(value_weight[layer], "expert", axis=0, tiled=True),
            lax.all_gather(output_weight[layer], "expert", axis=1, tiled=True),
        )
        query_lin = jnp.dot(own_rows, weight_q, preferred_element_type=jnp.float32).reshape(
            half_len, q_heads, head_dim
        )
        key_lin = jnp.dot(full_rows, weight_k, preferred_element_type=jnp.float32).reshape(
            length, kv_heads, head_dim
        )
        queries = rotate(query_lin, cos_own, sin_own, 1.0).astype(jnp.bfloat16)
        keys = rotate(key_lin, cosine, sine, 1.0).astype(jnp.bfloat16)
        values = (
            jnp.dot(full_rows, weight_v, preferred_element_type=jnp.float32)
            .astype(jnp.bfloat16)
            .reshape(length, kv_heads, head_dim)
        )
        grouped = queries.reshape(nblocks, block, kv_heads, share, head_dim)

        def attend(item):
            q_block, index = item
            scores = block_scores(q_block, keys, index)
            peak = jnp.max(scores, axis=-1, keepdims=True)
            weights = jnp.exp(scores - peak)
            total = jnp.sum(weights, axis=-1, keepdims=True)
            probs = (weights / total).astype(jnp.bfloat16)
            mixed_heads = jnp.einsum(
                "cgqk,kcd->qcgd", probs, values, preferred_element_type=jnp.float32
            )
            return (mixed_heads.astype(jnp.bfloat16), (peak + jnp.log(total))[..., 0])

        heads_out, log_totals = lax.map(attend, (grouped, block_ids))
        heads_flat = heads_out.reshape(half_len, q_heads * head_dim)
        summed = lax.psum(
            jnp.dot(heads_flat, weight_o, preferred_element_type=jnp.float32).astype(jnp.bfloat16),
            "head",
        ).astype(jnp.float32)
        attn_rows = lax.dynamic_slice_in_dim(summed, lax.axis_index("head") * rows, rows, 0)
        middle = current + attn_rows
        scale_two = rms_scale(middle)
        normed_two = (middle * scale_two * mixture_gain[layer]).astype(jnp.bfloat16)
        logits = jnp.dot(normed_two, router_weight[layer], preferred_element_type=jnp.float32)
        hits = routes[layer][:, :, None] == expert_ids[None, None, :]
        chosen = jnp.sum(jnp.where(hits, logits[:, None, :], 0.0), axis=-1)
        gates = jax.nn.softmax(chosen, axis=-1)
        slot_of, owner_of = slot_tables(
            hits.reshape(count, all_experts).astype(jnp.int32), capacity
        )
        valid = owner_of < count
        safe_owner = jnp.minimum(owner_of, count - 1)
        send = jnp.where(
            valid[:, None],
            jnp.take(normed_two, safe_owner // top, axis=0),
            jnp.zeros((), jnp.bfloat16),
        )
        send = send.reshape(owners, local_experts, capacity, width)
        received = lax.all_to_all(send, "expert", split_axis=0, concat_axis=0, tiled=True)
        mixed = jnp.einsum(
            "nerd,edf->nerf", received, expert_in[layer], preferred_element_type=jnp.float32
        )
        gate_part = mixed[..., :hidden_width]
        up_part = mixed[..., hidden_width:]
        hidden = (jax.nn.silu(gate_part) * up_part).astype(jnp.bfloat16)
        expert_y = jnp.einsum(
            "nerf,efd->nerd", hidden, expert_out[layer], preferred_element_type=jnp.float32
        ).astype(jnp.bfloat16)
        returned = lax.all_to_all(
            expert_y, "expert", split_axis=0, concat_axis=0, tiled=True
        ).reshape(all_experts * capacity, width)
        picked = jnp.take(returned, slot_of, axis=0).reshape(rows, top, width)
        after = middle + jnp.sum(gates[..., None] * picked, axis=1)
        saved.append(
            (
                current,
                scale_one,
                own_rows,
                weight_q,
                weight_k,
                weight_v,
                weight_o,
                grouped,
                keys,
                values,
                heads_flat,
                log_totals,
                middle,
                scale_two,
                normed_two,
                hits,
                gates,
                slot_of,
                valid,
                safe_owner,
                received,
                gate_part,
                up_part,
                hidden,
                picked,
            )
        )
        current = after
    outputs = current.astype(jnp.bfloat16)
    grad = cotangent.astype(jnp.float32)
    gain_a_list, gain_m_list, router_list = ([], [], [])
    query_list, key_list, value_list, out_list, in_list, down_list = ([], [], [], [], [], [])
    for layer in reversed(range(layers)):
        (
            state_in,
            scale_one,
            own_rows,
            weight_q,
            weight_k,
            weight_v,
            weight_o,
            grouped,
            keys,
            values,
            heads_flat,
            log_totals,
            middle,
            scale_two,
            normed_two,
            hits,
            gates,
            slot_of,
            valid,
            safe_owner,
            received,
            gate_part,
            up_part,
            hidden,
            picked,
        ) = saved[layer]
        dgates = jnp.sum(grad[:, None, :] * picked, axis=-1)
        dpicked = (gates[..., None] * grad[:, None, :]).astype(jnp.bfloat16).reshape(count, width)
        send_grad = jnp.where(
            valid[:, None], jnp.take(dpicked, safe_owner, axis=0), jnp.zeros((), jnp.bfloat16)
        )
        send_grad = send_grad.reshape(owners, local_experts, capacity, width)
        dexpert = lax.all_to_all(send_grad, "expert", split_axis=0, concat_axis=0, tiled=True)
        dhidden = jnp.einsum(
            "nerd,efd->nerf", dexpert, expert_out[layer], preferred_element_type=jnp.float32
        )
        grad_down = jnp.einsum(
            "nerf,nerd->efd", hidden, dexpert, preferred_element_type=jnp.float32
        )
        sigma = jax.nn.sigmoid(gate_part)
        dgate = dhidden * up_part * sigma * (1.0 + gate_part * (1.0 - sigma))
        dup = dhidden * (gate_part * sigma)
        dmixed = jnp.concatenate([dgate, dup], axis=-1).astype(jnp.bfloat16)
        grad_in_w = jnp.einsum(
            "nerd,nerf->edf", received, dmixed, preferred_element_type=jnp.float32
        )
        dinput_rows = jnp.einsum(
            "nerf,edf->nerd", dmixed, expert_in[layer], preferred_element_type=jnp.float32
        ).astype(jnp.bfloat16)
        dback = lax.all_to_all(
            dinput_rows, "expert", split_axis=0, concat_axis=0, tiled=True
        ).reshape(all_experts * capacity, width)
        dnormed_two = jnp.sum(
            jnp.take(dback, slot_of, axis=0).reshape(rows, top, width), axis=1, dtype=jnp.float32
        )
        dchosen = gates * (dgates - jnp.sum(gates * dgates, axis=-1, keepdims=True))
        dlogits = jnp.sum(jnp.where(hits, dchosen[..., None], 0.0), axis=1)
        dnormed_two = dnormed_two + jnp.dot(
            dlogits, router_weight[layer].astype(jnp.float32).T, precision=HIGH
        )
        router_list.insert(0, jnp.dot(normed_two.astype(jnp.float32).T, dlogits, precision=HIGH))
        dmiddle, gain_m = norm_back(middle, scale_two, mixture_gain[layer], dnormed_two)
        gain_m_list.insert(0, gain_m)
        dmiddle = grad + dmiddle
        full_dattn = lax.all_gather(dmiddle.astype(jnp.bfloat16), "head", axis=0, tiled=True)
        grad_o = contract_rows(heads_flat, full_dattn)
        dheads = contract_cols(full_dattn, weight_o).astype(jnp.bfloat16)
        dgrouped = dheads.reshape(nblocks, block, kv_heads, share, head_dim)

        def attend_back(carry, item):
            key_acc, value_acc = carry
            q_block, d_block, lse_block, index = item
            scores = block_scores(q_block, keys, index)
            probs = jnp.exp(scores - lse_block[..., None])
            dprobs = jnp.einsum(
                "qcgd,kcd->cgqk", d_block, values, preferred_element_type=jnp.float32
            )
            delta = jnp.sum(probs * dprobs, axis=-1, keepdims=True)
            dscores = (probs * (dprobs - delta)).astype(jnp.bfloat16)
            dquery = (
                jnp.einsum("cgqk,kcd->qcgd", dscores, keys, preferred_element_type=jnp.float32)
                * factor
            )
            key_acc = (
                key_acc
                + jnp.einsum("cgqk,qcgd->kcd", dscores, q_block, preferred_element_type=jnp.float32)
                * factor
            )
            value_acc = value_acc + jnp.einsum(
                "cgqk,qcgd->kcd",
                probs.astype(jnp.bfloat16),
                d_block,
                preferred_element_type=jnp.float32,
            )
            return ((key_acc, value_acc), dquery.reshape(block, q_heads, head_dim))

        empty = jnp.zeros((length, kv_heads, head_dim), jnp.float32)
        (dkeys_all, dvalues_all), dqueries = lax.scan(
            attend_back, (empty, empty), (grouped, dgrouped, log_totals, block_ids)
        )
        dkeys, dvalues = (
            lax.psum_scatter(
                dkeys_all.reshape(length, kv_heads * head_dim).astype(jnp.bfloat16),
                "dp",
                scatter_dimension=0,
                tiled=True,
            ).astype(jnp.float32),
            lax.psum_scatter(
                dvalues_all.reshape(length, kv_heads * head_dim).astype(jnp.bfloat16),
                "dp",
                scatter_dimension=0,
                tiled=True,
            ).astype(jnp.float32),
        )
        dquery_lin = (
            rotate(dqueries.reshape(half_len, q_heads, head_dim), cos_own, sin_own, -1.0)
            .astype(jnp.bfloat16)
            .reshape(half_len, q_heads * head_dim)
        )
        dkey_lin = (
            rotate(dkeys.reshape(half_len, kv_heads, head_dim), cos_own, sin_own, -1.0)
            .astype(jnp.bfloat16)
            .reshape(half_len, kv_heads * head_dim)
        )
        dvalue_lin = dvalues.astype(jnp.bfloat16)
        grad_q = contract_rows(own_rows, dquery_lin)
        grad_k = contract_rows(own_rows, dkey_lin)
        grad_v = contract_rows(own_rows, dvalue_lin)
        part_q = contract_cols(dquery_lin, weight_q)
        part_k = contract_cols(dkey_lin, weight_k)
        part_v = contract_cols(dvalue_lin, weight_v)
        dnormed_one = lax.psum_scatter(
            (part_q + part_k + part_v).astype(jnp.bfloat16), "head", scatter_dimension=0, tiled=True
        ).astype(jnp.float32)
        dstate, gain_a = norm_back(state_in, scale_one, attention_gain[layer], dnormed_one)
        gain_a_list.insert(0, gain_a)
        grad = dmiddle + dstate
        shard_q, shard_k, shard_v, shard_o = (
            *side_by_side(
                (
                    grad_q.astype(jnp.bfloat16),
                    grad_k.astype(jnp.bfloat16),
                    grad_v.astype(jnp.bfloat16),
                ),
                ("dp", "expert"),
                0,
                1,
            ),
            sum_at_owner(grad_o.astype(jnp.bfloat16), ("dp", "expert"), 1),
        )
        shard_in, shard_down = (
            lax.psum_scatter(
                grad_in_w.astype(jnp.bfloat16), ("dp", "head"), scatter_dimension=1, tiled=True
            ).astype(jnp.float32),
            lax.psum_scatter(
                grad_down.astype(jnp.bfloat16), ("dp", "head"), scatter_dimension=1, tiled=True
            ).astype(jnp.float32),
        )
        query_list.insert(0, shard_q)
        key_list.insert(0, shard_k)
        value_list.insert(0, shard_v)
        out_list.insert(0, shard_o)
        in_list.insert(0, shard_in)
        down_list.insert(0, shard_down)
    total_a, total_m, total_r = lax.psum(
        (jnp.stack(gain_a_list), jnp.stack(gain_m_list), jnp.stack(router_list)),
        ("dp", "expert", "head"),
    )
    return (
        outputs,
        grad,
        total_a,
        total_m,
        jnp.stack(query_list),
        jnp.stack(key_list),
        jnp.stack(value_list),
        jnp.stack(out_list),
        total_r,
        jnp.stack(in_list),
        jnp.stack(down_list),
    )


def solution(mesh):
    in_specs = (
        P(("dp", "expert", "head"), None),
        P(("dp", "expert", "head"), None),
        P("expert", None),
        P(None, ("dp", "expert", "head"), None),
        P(),
        P(),
        P(None, "expert", "head"),
        P(None, "expert", "head"),
        P(None, "expert", "head"),
        P(None, "head", "expert"),
        P(),
        P(None, "expert", None, None),
        P(None, "expert", None, None),
    )
    out_specs = (
        P(("dp", "expert", "head"), None),
        P(("dp", "expert", "head"), None),
        P(),
        P(),
        P(None, ("dp", "expert"), "head"),
        P(None, ("dp", "expert"), "head"),
        P(None, ("dp", "expert"), "head"),
        P(None, "head", ("dp", "expert")),
        P(),
        P(None, "expert", ("dp", "head"), None),
        P(None, "expert", ("dp", "head"), None),
    )
    return jax.shard_map(
        per_device, mesh=mesh, in_specs=in_specs, out_specs=out_specs, check_vma=False
    )
```

profile of v0, /device:TPU:0, one launch (start us, length us, event | category | flops | bytes accessed | tf_op | source)
XLA Modules:
  0.0 1667.1 jit_solution(1662314493783846153)
XLA Ops:
  13.2 9.0 reduce-window.14
  27.7 15.6 all-gather
  44.0 14.5 all-gather.1
  61.0 16.4 all-gather.3
  78.1 14.8 all-gather.2
  107.4 4.6 scatter_custom_fusion
  112.6 48.2 %all-reduce.5.cloned.1.call-done = bf16[512,1024]{1,0:T(8,128)(2,1)} async-done(((bf16[512,1024]{1,0:T(8,128)(2,1)}), bf16[512,1024]{1,0:T(8,128)(2,1)}) %all-reduce.5.cloned.1.call-update) | async-done | bytes 1048592 | tf_op jit(solution)/shard_map/psum | solution.py:188
  163.0 4.9 gather_fusion
  178.2 55.3 %all_to_all.60 = bf16[4,8,34,1024]{3,1,2,0:T(8,128)(2,1)} all-to-all(bf16[4,8,34,1024]{3,1,2,0:T(8,128)(2,1)S(1)} %copy.120), channel_id=1, replica_groups=mesh['dp'=2,'expert'=4,'head'=4] {'expert'}, dimensions={0} | all-to-all | bytes 4456448 | tf_op jit(solution)/shard_map/all_to_all | solution.py:211
  233.6 12.2 fusion.73
  248.1 5.4 convert_bitcast_fusion.5
  256.1 4.6 all-to-all-start.1
  260.8 11.1 all-gather.15.cloned.1.call-start
  273.4 37.5 %all-to-all-done.1 = bf16[4,8,34,1024]{3,1,2,0:T(8,128)(2,1)} async-done(((bf16[4,8,34,1024]{3,1,2,0:T(8,128)(2,1)}), bf16[4,8,34,1024]{3,1,2,0:T(8,128)(2,1)}, u32[]{:S(2)}, u32[]{:S(2)}) %all-to-all-start.1) | async-done | bytes 2228256 | tf_op jit(solution)/shard_map/all_to_all | solution.py:221
  318.0 5.3 gather_fusion.1
  329.0 9.0 reduce-window.16
  339.0 13.9 all-gather.4
  352.8 14.5 all-gather.5
  367.3 17.0 %all-gather.7 = bf16[1,256,1024]{2,1,0:T(8,128)(2,1)} all-gather(bf16[1,256,256]{2,1,0:T(8,128)(2,1)S(1)} %copy-done.75), channel_id=9, replica_groups=mesh['dp'=2,'expert'=4,'head'=4] {'expert'}, dimensions={2}, use_global_device_ids=true | all-gather | bytes 655360 | tf_op jit(solution)/shard_map/all_gather | solution.py:157
  384.3 14.7 all-gather.6
  419.5 43.1 %all-reduce.7.cloned.1.call-done = bf16[512,1024]{1,0:T(8,128)(2,1)} async-done(((bf16[512,1024]{1,0:T(8,128)(2,1)}), bf16[512,1024]{1,0:T(8,128)(2,1)}) %all-reduce.7.cloned.1.call-update) | async-done | bytes 1048592 | tf_op jit(solution)/shard_map/psum | solution.py:188
  464.4 4.5 gather_fusion.2
  478.6 55.6 %all_to_all.61 = bf16[4,8,34,1024]{3,1,2,0:T(8,128)(2,1)} all-to-all(bf16[4,8,34,1024]{3,1,2,0:T(8,128)(2,1)S(1)} %copy.130), channel_id=1, replica_groups=mesh['dp'=2,'expert'=4,'head'=4] {'expert'}, dimensions={0} | all-to-all | bytes 4456448 | tf_op jit(solution)/shard_map/all_to_all | solution.py:211
  534.1 12.0 fusion.68
  548.4 5.4 convert_bitcast_fusion.4
  565.8 44.6 %all-to-all-done.3 = bf16[4,8,34,1024]{3,1,2,0:T(8,128)(2,1)S(1)} async-done(((bf16[4,8,34,1024]{3,1,2,0:T(8,128)(2,1)}), bf16[4,8,34,1024]{3,1,2,0:T(8,128)(2,1)S(1)}, u32[]{:S(2)}, u32[]{:S(2)}) %all-to-all-start.3) | async-done | bytes 2228256 | tf_op jit(solution)/shard_map/all_to_all | solution.py:221
  616.0 5.4 gather_fusion.3
  625.7 4.9 gather_fusion.4
  638.0 53.2 %all_to_all.62 = bf16[4,8,34,1024]{3,1,2,0:T(8,128)(2,1)S(1)} all-to-all(bf16[4,8,34,1024]{3,1,2,0:T(8,128)(2,1)S(1)} %copy.135), channel_id=1, replica_groups=mesh['dp'=2,'expert'=4,'head'=4] {'expert'}, dimensions={0} | all-to-all | bytes 4456448 | tf_op jit(solution)/shard_map/all_to_all | solution.py:294
  691.2 10.2 fusion.56
  701.4 10.1 convert_bitcast_fusion.3
  718.2 49.7 %all-to-all-done.5 = bf16[4,8,34,1024]{3,1,2,0:T(8,128)(2,1)S(1)} async-done(((bf16[4,8,34,1024]{3,1,2,0:T(8,128)(2,1)}), bf16[4,8,34,1024]{3,1,2,0:T(8,128)(2,1)S(1)}, u32[]{:S(2)}, u32[]{:S(2)}) %all-to-all-start.5) | async-done | bytes 2228256 | tf_op jit(solution)/shard_map/all_to_all | solution.py:311
  773.4 5.3 gather_fusion.5
  778.8 5.3 convert_reduce_fusion.1
  787.0 24.7 %all-gather.17.cloned.1.call-done = bf16[512,1024]{1,0:T(8,128)(2,1)} async-done(((bf16[128,1024]{1,0:T(8,128)(2,1)}), bf16[512,1024]{1,0:T(8,128)(2,1)}) %all-gather.17.cloned.1.call-update) | async-done | bytes 1048592 | tf_op jit(solution)/shard_map/all_gather | solution.py:326
  813.5 5.3 fusion.19
  825.7 5.5 fusion.100
  836.8 7.4 reduce-scatter.13.cloned.1.call-done
  848.3 28.5 %reduce-scatter.15.cloned.1.call-done = bf16[128,1024]{1,0:T(8,128)(2,1)} async-done(((bf16[512,1024]{1,0:T(8,128)(2,1)}), bf16[128,1024]{1,0:T(8,128)(2,1)}) %reduce-scatter.15.cloned.1.call-update) | async-done | bytes 262160 | tf_op jit(solution)/shard_map/reduce_scatter | solution.py:393
  884.4 4.9 gather_fusion.6
  896.3 55.7 %all_to_all.63 = bf16[4,8,34,1024]{3,1,2,0:T(8,128)(2,1)S(1)} all-to-all(bf16[4,8,34,1024]{3,1,2,0:T(8,128)(2,1)S(1)} %copy.145), channel_id=1, replica_groups=mesh['dp'=2,'expert'=4,'head'=4] {'expert'}, dimensions={0} | all-to-all | bytes 4456448 | tf_op jit(solution)/shard_map/all_to_all | solution.py:294
  952.0 10.2 fusion.52
  962.3 10.1 convert_bitcast_fusion.2
  979.1 49.5 %all-to-all-done.7 = bf16[4,8,34,1024]{3,1,2,0:T(8,128)(2,1)S(1)} async-done(((bf16[4,8,34,1024]{3,1,2,0:T(8,128)(2,1)}), bf16[4,8,34,1024]{3,1,2,0:T(8,128)(2,1)S(1)}, u32[]{:S(2)}, u32[]{:S(2)}) %all-to-all-start.7) | async-done | bytes 2228256 | tf_op jit(solution)/shard_map/all_to_all | solution.py:311
  1034.2 5.3 gather_fusion.7
  1045.8 24.7 %all-gather.19.cloned.1.call-done = bf16[512,1024]{1,0:T(8,128)(2,1)} async-done(((bf16[128,1024]{1,0:T(8,128)(2,1)}), bf16[512,1024]{1,0:T(8,128)(2,1)}) %all-gather.19.cloned.1.call-update) | async-done | bytes 1048592 | tf_op jit(solution)/shard_map/all_gather | solution.py:326
  1072.2 5.3 fusion.12
  1084.4 5.5 fusion.97
  1095.3 7.8 reduce-scatter.19.cloned.1.call-done
  1107.3 9.1 bitcast_convert_fusion.2
  1117.9 8.3 bitcast_convert_fusion.3
  1127.8 12.2 bitcast_convert_fusion
  1141.7 14.1 bitcast_convert_fusion.1
  1158.7 4.9 all-to-all-start.11
  1166.7 11.7 all-to-all-done.11
  1185.3 23.4 %all-to-all-done.9 = bf16[8,128,512]{1,2,0:T(8,128)(2,1)} async-done(((bf16[8,128,512]{1,2,0:T(8,128)(2,1)}), bf16[8,128,512]{1,2,0:T(8,128)(2,1)}, u32[]{:S(2)}, u32[]{:S(2)}) %all-to-all-start.9) | async-done | bytes 1048608 | tf_op jit(solution)/shard_map/all_to_all | solution.py:24
  1215.2 12.4 all-to-all-done.10
  1237.0 20.1 %all-to-all-done.8 = bf16[8,128,512]{1,2,0:T(8,128)(2,1)S(1)} async-done(((bf16[8,128,512]{1,2,0:T(8,128)(2,1)}), bf16[8,128,512]{1,2,0:T(8,128)(2,1)S(1)}, u32[]{:S(2)}, u32[]{:S(2)}) %all-to-all-start.8) | async-done | bytes 1048608 | tf_op jit(solution)/shard_map/all_to_all | solution.py:24
  1261.1 39.1 %all-reduce = (f32[2,1024]{1,0:T(2,128)}, f32[2,1024]{1,0:T(2,128)}) all-reduce(f32[2,1024]{1,0:T(2,128)S(1)} %get-tuple-element.250, f32[2,1024]{1,0:T(2,128)S(1)} %get-tuple-element.251), channel_id=1, replica_groups=mesh['dp'=2,'expert'=4,'head'=4] {'dp','expert','head'}, use_global_device_ids=true, to_apply=%region_51.55 | all-reduce | flops 4096 | bytes 32768 | tf_op jit(solution)/shard_map/psum | solution.py:426
  1302.5 4.5 maximum_convert_fusion.1
  1306.9 99.4 %reduce-scatter.25.cloned.1.call-done = bf16[8,128,1024]{2,1,0:T(8,128)(2,1)} async-done(((bf16[8,1024,1024]{2,1,0:T(8,128)(2,1)}), bf16[8,128,1024]{2,1,0:T(8,128)(2,1)}) %reduce-scatter.25.cloned.1.call-update) | async-done | bytes 2097168 | tf_op jit(solution)/shard_map/reduce_scatter | solution.py:413
  1406.3 119.6 %reduce-scatter.23.cloned.1.call-done = bf16[8,128,1024]{2,1,0:T(8,128)(2,1)} async-done(((bf16[8,1024,1024]{2,1,0:T(8,128)(2,1)}), bf16[8,128,1024]{2,1,0:T(8,128)(2,1)}) %reduce-scatter.23.cloned.1.call-update) | async-done | bytes 2097168 | tf_op jit(solution)/shard_map/reduce_scatter | solution.py:413
  1525.9 6.2 maximum_convert_fusion
  1532.1 126.3 %all-reduce.9.cloned.1.call-done = f32[2,1024,32]{1,2,0:T(8,128)} async-done(((f32[2,1024,32]{1,2,0:T(8,128)}), f32[2,1024,32]{1,2,0:T(8,128)}) %all-reduce.9.cloned.1.call-update) | async-done | bytes 262160 | tf_op jit(solution)/shard_map/psum | solution.py:426
  (585 shorter events, 250.9 us)
Async XLA Ops:
  7.2 86.5 %all-gather.13.cloned.1.call-start = ((), (), s32[]{:S(2)}) async-start(), calls=%async_computation.22 | async-start | bytes 2359296 | tf_op jit(solution)/shard_map/all_gather | solution.py:151
  8.3 35.0 %copy-start.93 = (bf16[2,256,128]{2,1,0:T(8,128)(2,1)S(1)}, bf16[2,256,128]{2,1,0:T(8,128)(2,1)}, u32[]{:S(2)}) copy-start(bf16[2,256,128]{2,1,0:T(8,128)(2,1)} %param.26) | copy-start | bytes 393220
  11.6 149.3 %all-reduce.5.cloned.1.call-start = ((), (), s32[]{:S(2)}) async-start(), calls=%async_computation.23 | async-start | bytes 2097152 | tf_op jit(solution)/shard_map/psum | solution.py:188
  12.9 259.2 %copy-start.104 = (s32[128,8]{0,1:T(8,128)}, s32[128,8]{0,1:T(8,128)S(1)}, u32[]{:S(2)}) copy-start(s32[128,8]{0,1:T(8,128)S(1)} %get-tuple-element.231) | copy-start | bytes 12292
  24.7 35.6 %copy-start.82 = (bf16[2,256,256]{2,1,0:T(8,128)(2,1)S(1)}, bf16[2,256,256]{2,1,0:T(8,128)(2,1)}, u32[]{:S(2)}) copy-start(bf16[2,256,256]{2,1,0:T(8,128)(2,1)} %param.28) | copy-start | bytes 786436
  25.7 51.7 %copy-start.83 = (bf16[2,256,256]{2,1,0:T(8,128)(2,1)S(1)}, bf16[2,256,256]{2,1,0:T(8,128)(2,1)}, u32[]{:S(2)}) copy-start(bf16[2,256,256]{2,1,0:T(8,128)(2,1)} %param.25) | copy-start | bytes 786436
  43.3 57.4 %copy-start.29 = (bf16[1,1024,128]{2,1,0:T(8,128)(2,1)}, bf16[1,1024,128]{2,1,0:T(8,128)(2,1)S(1)}, u32[]{:S(2)}) copy-start(bf16[1,1024,128]{2,1,0:T(8,128)(2,1)S(1)} %all-gather) | copy-start | bytes 786436
  58.5 37.8 %copy-start.35 = (bf16[1,1024,128]{2,1,0:T(8,128)(2,1)}, bf16[1,1024,128]{2,1,0:T(8,128)(2,1)S(1)}, u32[]{:S(2)}) copy-start(bf16[1,1024,128]{2,1,0:T(8,128)(2,1)S(1)} %all-gather.1) | copy-start | bytes 786436
  59.5 37.4 %copy-start.27 = (f32[1024,64]{0,1:T(8,128)}, f32[1024,64]{0,1:T(8,128)S(1)}, u32[]{:S(2)}) copy-start(f32[1024,64]{0,1:T(8,128)S(1)} %get-tuple-element.227) | copy-start | bytes 786436
  59.6 343.1 %copy-start.14 = (f32[512,64]{0,1:T(8,128)}, f32[512,64]{0,1:T(8,128)S(1)}, u32[]{:S(2)}) copy-start(f32[512,64]{0,1:T(8,128)S(1)} %constant_dynamic-slice_fusion.1) | copy-start | bytes 393220
  77.4 27.1 %copy-start.47 = (bf16[1,256,1024]{2,1,0:T(8,128)(2,1)}, bf16[1,256,1024]{2,1,0:T(8,128)(2,1)S(1)}, u32[]{:S(2)}) copy-start(bf16[1,256,1024]{2,1,0:T(8,128)(2,1)S(1)} %all-gather.3) | copy-start | bytes 1572868
  104.5 56.3 %copy-start.10 = (bf16[128,1024]{1,0:T(8,128)(2,1)S(1)}, bf16[128,1024]{1,0:T(8,128)(2,1)}, u32[]{:S(2)}) copy-start(bf16[128,1024]{1,0:T(8,128)(2,1)} %param.19) | copy-start | bytes 786436
  107.4 216.0 %copy-start.124 = (pred[1024]{0:T(1024)(128)(4,1)}, pred[1024]{0:T(1024)(128)(4,1)S(1)}, u32[]{:S(2)}) copy-start(pred[1024]{0:T(1024)(128)(4,1)S(1)} %get-tuple-element.190) | copy-start | bytes 3076
  112.6 55.4 %copy-start.116 = (pred[1088]{0:T(1024)(128)(4,1)}, pred[1088]{0:T(1024)(128)(4,1)S(1)}, u32[]{:S(2)}) copy-start(pred[1088]{0:T(1024)(128)(4,1)S(1)} %get-tuple-element.239) | copy-start | bytes 3268
  112.6 55.3 %copy-start.94 = (f32[1,1024]{1,0:T(1,128)}, f32[1,1024]{1,0:T(1,128)S(1)}, u32[]{:S(2)}) copy-start(f32[1,1024]{1,0:T(1,128)S(1)} %get-tuple-element.236) | copy-start | bytes 12292
  163.0 108.9 %copy-start = (bf16[128,1024]{1,0:T(8,128)(2,1)}, bf16[128,1024]{1,0:T(8,128)(2,1)S(1)}, u32[]{:S(2)}) copy-start(bf16[128,1024]{1,0:T(8,128)(2,1)S(1)} %multiply_convert_fusion.4) | copy-start | bytes 786436
  256.1 54.7 %all-to-all-start.1 = ((bf16[4,8,34,1024]{3,1,2,0:T(8,128)(2,1)}), bf16[4,8,34,1024]{3,1,2,0:T(8,128)(2,1)}, u32[]{:S(2)}, u32[]{:S(2)}) async-start(bf16[4,8,34,1024]{3,1,2,0:T(8,128)(2,1)} %copy.122), calls=%async_computation.1 | async-start | bytes 4456448 | tf_op jit(solution)/shard_map/all_to_all | solution.py:221
  260.8 138.2 %all-gather.15.cloned.1.call-start = ((), (), s32[]{:S(2)}) async-start(), calls=%async_computation.24 | async-start | bytes 2359296 | tf_op jit(solution)/shard_map/all_gather | solution.py:151
  271.9 46.1 %copy-start.102 = (s32[1024]{0:T(1024)}, s32[1024]{0:T(1024)S(1)}, u32[]{:S(2)}) copy-start(s32[1024]{0:T(1024)S(1)} %broadcast_clamp_fusion.1) | copy-start | bytes 12292
  273.4 50.0 %copy-start.72 = (f32[128,8]{1,0:T(8,128)}, f32[128,8]{1,0:T(8,128)S(1)}, u32[]{:S(2)}) copy-start(f32[128,8]{1,0:T(8,128)S(1)} %copy.115) | copy-start | bytes 12292
  326.5 40.8 %copy-start.75 = (bf16[1,256,256]{2,1,0:T(8,128)(2,1)S(1)}, bf16[1,256,256]{2,1,0:T(8,128)(2,1)}, u32[]{:S(2)}) copy-start(bf16[1,256,256]{2,1,0:T(8,128)(2,1)} %get-tuple-element.218) | copy-start | bytes 393220
  326.5 57.7 %copy-start.76 = (bf16[1,256,256]{2,1,0:T(8,128)(2,1)S(1)}, bf16[1,256,256]{2,1,0:T(8,128)(2,1)}, u32[]{:S(2)}) copy-start(bf16[1,256,256]{2,1,0:T(8,128)(2,1)} %get-tuple-element.220) | copy-start | bytes 393220
  328.6 134.0 %all-reduce.7.cloned.1.call-start = ((), (), s32[]{:S(2)}) async-start(), calls=%async_computation.25 | async-start | bytes 2097152 | tf_op jit(solution)/shard_map/psum | solution.py:188
  352.8 53.3 %copy-start.31 = (bf16[1,1024,128]{2,1,0:T(8,128)(2,1)}, bf16[1,1024,128]{2,1,0:T(8,128)(2,1)S(1)}, u32[]{:S(2)}) copy-start(bf16[1,1024,128]{2,1,0:T(8,128)(2,1)S(1)} %all-gather.4) | copy-start | bytes 786436
  367.3 31.6 %copy-start.39 = (bf16[1,1024,128]{2,1,0:T(8,128)(2,1)}, bf16[1,1024,128]{2,1,0:T(8,128)(2,1)S(1)}, u32[]{:S(2)}) copy-start(bf16[1,1024,128]{2,1,0:T(8,128)(2,1)S(1)} %all-gather.5) | copy-start | bytes 786436
  464.4 99.2 %copy-start.2 = (bf16[128,1024]{1,0:T(8,128)(2,1)}, bf16[128,1024]{1,0:T(8,128)(2,1)S(1)}, u32[]{:S(2)}) copy-start(bf16[128,1024]{1,0:T(8,128)(2,1)S(1)} %multiply_convert_fusion.2) | copy-start | bytes 786436
  556.4 54.0 %all-to-all-start.3 = ((bf16[4,8,34,1024]{3,1,2,0:T(8,128)(2,1)}), bf16[4,8,34,1024]{3,1,2,0:T(8,128)(2,1)S(1)}, u32[]{:S(2)}, u32[]{:S(2)}) async-start(bf16[4,8,34,1024]{3,1,2,0:T(8,128)(2,1)} %copy.132), calls=%async_computation.3 | async-start | bytes 4456448 | tf_op jit(solution)/shard_map/all_to_all | solution.py:221
  565.3 45.1 %copy-start.140 = (f32[128]{0:T(128)}, f32[128]{0:T(128)S(1)}, u32[]{:S(2)}) copy-start(f32[128]{0:T(128)S(1)} %reduce_max.41) | copy-start | bytes 1540
  714.1 53.7 %all-to-all-start.5 = ((bf16[4,8,34,1024]{3,1,2,0:T(8,128)(2,1)}), bf16[4,8,34,1024]{3,1,2,0:T(8,128)(2,1)S(1)}, u32[]{:S(2)}, u32[]{:S(2)}) async-start(bf16[4,8,34,1024]{3,1,2,0:T(8,128)(2,1)} %copy.137), calls=%async_computation.5 | async-start | bytes 4456448 | tf_op jit(solution)/shard_map/all_to_all | solution.py:311
  717.9 93.8 %all-gather.17.cloned.1.call-start = ((), (), s32[]{:S(2)}) async-start(), calls=%async_computation.26 | async-start | bytes 1310720 | tf_op jit(solution)/shard_map/all_gather | solution.py:326
  718.2 65.8 %copy-start.86 = (f32[128,32]{0,1:T(8,128)}, f32[128,32]{0,1:T(8,128)S(1)}, u32[]{:S(2)}) copy-start(f32[128,32]{0,1:T(8,128)S(1)} %select_reduce_fusion.1) | copy-start | bytes 49156
  784.0 27.7 %copy-start.50 = (bf16[1,256,1024]{2,1,0:T(8,128)(2,1)S(1)}, bf16[1,256,1024]{2,1,0:T(8,128)(2,1)}, u32[]{:S(2)}) copy-start(bf16[1,256,1024]{2,1,0:T(8,128)(2,1)} %all-gather.7) | copy-start | bytes 1572868
  784.1 29.4 %copy-start.60 = (bf16[1024,128]{0,1:T(8,128)(2,1)S(1)}, bf16[1024,128]{0,1:T(8,128)(2,1)}, u32[]{:S(2)}) copy-start(bf16[1024,128]{0,1:T(8,128)(2,1)} %copy-done.59) | copy-start | bytes 786436
  785.2 33.6 %copy-start.145 = (f32[128]{0:T(128)}, f32[128]{0:T(128)S(1)}, u32[]{:S(2)}) copy-start(f32[128]{0:T(128)S(1)} %broadcast_multiply_fusion.5) | copy-start | bytes 1540
  787.0 45.6 %reduce-scatter.11.cloned.1.call-start = ((), (), s32[]{:S(2)}) async-start(), calls=%async_computation.27 | async-start | bytes 393216 | tf_op jit(solution)/shard_map/reduce_scatter | solution.py:363
  824.7 19.6 %reduce-scatter.13.cloned.1.call-start = ((), (), s32[]{:S(2)}) async-start(), calls=%async_computation.28 | async-start | bytes 393216 | tf_op jit(solution)/shard_map/reduce_scatter | solution.py:369
  831.2 45.6 %reduce-scatter.15.cloned.1.call-start = ((), (), s32[]{:S(2)}) async-start(), calls=%async_computation.29 | async-start | bytes 1310720 | tf_op jit(solution)/shard_map/reduce_scatter | solution.py:393
  845.7 32.9 %copy-start.34 = (bf16[128,1024]{1,0:T(8,128)(2,1)S(1)}, bf16[128,1024]{1,0:T(8,128)(2,1)}, u32[]{:S(2)}) copy-start(bf16[128,1024]{1,0:T(8,128)(2,1)} %param.20) | copy-start | bytes 786436
  847.3 34.3 %copy-start.125 = (pred[1024]{0:T(1024)(128)(4,1)S(1)}, pred[1024]{0:T(1024)(128)(4,1)}, u32[]{:S(2)}) copy-start(pred[1024]{0:T(1024)(128)(4,1)} %copy-done.124) | copy-start | bytes 3076
  975.0 53.6 %all-to-all-start.7 = ((bf16[4,8,34,1024]{3,1,2,0:T(8,128)(2,1)}), bf16[4,8,34,1024]{3,1,2,0:T(8,128)(2,1)S(1)}, u32[]{:S(2)}, u32[]{:S(2)}) async-start(bf16[4,8,34,1024]{3,1,2,0:T(8,128)(2,1)} %copy.147), calls=%async_computation.10 | async-start | bytes 4456448 | tf_op jit(solution)/shard_map/all_to_all | solution.py:311
  978.6 91.8 %all-gather.19.cloned.1.call-start = ((), (), s32[]{:S(2)}) async-start(), calls=%async_computation.30 | async-start | bytes 1310720 | tf_op jit(solution)/shard_map/all_gather | solution.py:326
  979.1 63.6 %copy-start.88 = (f32[128,32]{0,1:T(8,128)}, f32[128,32]{0,1:T(8,128)S(1)}, u32[]{:S(2)}) copy-start(f32[128,32]{0,1:T(8,128)S(1)} %select_reduce_fusion) | copy-start | bytes 49156
  1039.6 30.9 %copy-start.48 = (bf16[1,256,1024]{2,1,0:T(8,128)(2,1)S(1)}, bf16[1,256,1024]{2,1,0:T(8,128)(2,1)}, u32[]{:S(2)}) copy-start(bf16[1,256,1024]{2,1,0:T(8,128)(2,1)} %copy-done.47) | copy-start | bytes 1572868
  1042.8 29.4 %copy-start.58 = (bf16[1024,128]{0,1:T(8,128)(2,1)S(1)}, bf16[1024,128]{0,1:T(8,128)(2,1)}, u32[]{:S(2)}) copy-start(bf16[1024,128]{0,1:T(8,128)(2,1)} %copy-done.57) | copy-start | bytes 786436
  1044.0 33.6 %copy-start.147 = (f32[128]{0:T(128)}, f32[128]{0:T(128)S(1)}, u32[]{:S(2)}) copy-start(f32[128]{0:T(128)S(1)} %broadcast_multiply_fusion.3) | copy-start | bytes 1540
  1045.7 45.6 %reduce-scatter.17.cloned.1.call-start = ((), (), s32[]{:S(2)}) async-start(), calls=%async_computation.31 | async-start | bytes 393216 | tf_op jit(solution)/shard_map/reduce_scatter | solution.py:363
  1083.4 19.6 %reduce-scatter.19.cloned.1.call-start = ((), (), s32[]{:S(2)}) async-start(), calls=%async_computation.32 | async-start | bytes 393216 | tf_op jit(solution)/shard_map/reduce_scatter | solution.py:369
  1089.9 169.8 %reduce-scatter.21.cloned.1.call-start = ((), (), s32[]{:S(2)}) async-start(), calls=%async_computation.33 | async-start | bytes 1310720 | tf_op jit(solution)/shard_map/reduce_scatter | solution.py:393
  1107.0 195.5 %reduce-scatter.29.cloned.1.call-start = ((), (), s32[]{:S(2)}) async-start(), calls=%async_computation.38 | async-start | bytes 9437184 | tf_op jit(solution)/shard_map/reduce_scatter | solution.py:416
  1116.3 186.1 %reduce-scatter.27.cloned.1.call-start = ((), (), s32[]{:S(2)}) async-start(), calls=%async_computation.37 | async-start | bytes 9437184 | tf_op jit(solution)/shard_map/reduce_scatter | solution.py:416
  1126.2 280.1 %reduce-scatter.25.cloned.1.call-start = ((), (), s32[]{:S(2)}) async-start(), calls=%async_computation.36 | async-start | bytes 18874368 | tf_op jit(solution)/shard_map/reduce_scatter | solution.py:413
  1140.1 385.9 %reduce-scatter.23.cloned.1.call-start = ((), (), s32[]{:S(2)}) async-start(), calls=%async_computation.35 | async-start | bytes 18874368 | tf_op jit(solution)/shard_map/reduce_scatter | solution.py:413
  1158.7 19.7 %all-to-all-start.11 = ((bf16[8,256,128]{2,1,0:T(8,128)(2,1)}), bf16[8,256,128]{2,1,0:T(8,128)(2,1)}, u32[]{:S(2)}, u32[]{:S(2)}) async-start(bf16[8,256,128]{2,1,0:T(8,128)(2,1)} %bitcast.476), calls=%async_computation.17 | async-start | bytes 1048576 | tf_op jit(solution)/shard_map/all_to_all | solution.py:24
  1166.7 46.1 %copy-start.7 = (bf16[1024,1024]{1,0:T(8,128)(2,1)S(1)}, bf16[1024,1024]{1,0:T(8,128)(2,1)}, u32[]{:S(2)}) copy-start(bf16[1024,1024]{1,0:T(8,128)(2,1)} %all-gather.13.cloned.1.call-done) | copy-start | bytes 6291460
  1178.4 30.3 %all-to-all-start.9 = ((bf16[8,128,512]{1,2,0:T(8,128)(2,1)}), bf16[8,128,512]{1,2,0:T(8,128)(2,1)}, u32[]{:S(2)}, u32[]{:S(2)}) async-start(bf16[8,128,512]{1,2,0:T(8,128)(2,1)} %copy_bitcast_fusion), calls=%async_computation.15 | async-start | bytes 2097152 | tf_op jit(solution)/shard_map/all_to_all | solution.py:24
  1184.4 28.9 %copy-start.78 = (bf16[512,128]{0,1:T(8,128)(2,1)S(1)}, bf16[512,128]{0,1:T(8,128)(2,1)}, u32[]{:S(2)}) copy-start(bf16[512,128]{0,1:T(8,128)(2,1)} %reduce-scatter.19.cloned.1.call-done) | copy-start | bytes 393220
  1184.4 29.2 %copy-start.56 = (bf16[512,128]{0,1:T(8,128)(2,1)S(1)}, bf16[512,128]{0,1:T(8,128)(2,1)}, u32[]{:S(2)}) copy-start(bf16[512,128]{0,1:T(8,128)(2,1)} %copy-done.55) | copy-start | bytes 393220
  1208.7 18.9 %all-to-all-start.10 = ((bf16[8,256,128]{2,1,0:T(8,128)(2,1)}), bf16[8,256,128]{2,1,0:T(8,128)(2,1)}, u32[]{:S(2)}, u32[]{:S(2)}) async-start(bf16[8,256,128]{2,1,0:T(8,128)(2,1)} %bitcast.475), calls=%async_computation.16 | async-start | bytes 1048576 | tf_op jit(solution)/shard_map/all_to_all | solution.py:24
  1227.6 29.5 %all-to-all-start.8 = ((bf16[8,128,512]{1,2,0:T(8,128)(2,1)}), bf16[8,128,512]{1,2,0:T(8,128)(2,1)S(1)}, u32[]{:S(2)}, u32[]{:S(2)}) async-start(bf16[8,128,512]{1,2,0:T(8,128)(2,1)} %copy_bitcast_fusion.1), calls=%async_computation.14 | async-start | bytes 2097152 | tf_op jit(solution)/shard_map/all_to_all | solution.py:24
  1231.2 427.2 %all-reduce.9.cloned.1.call-start = ((), (), s32[]{:S(2)}) async-start(), calls=%async_computation.34 | async-start | bytes 524288 | tf_op jit(solution)/shard_map/psum | solution.py:426
  1236.3 63.9 %copy-start.24 = (f32[128,1024]{1,0:T(8,128)S(1)}, f32[128,1024]{1,0:T(8,128)}, u32[]{:S(2)}) copy-start(f32[128,1024]{1,0:T(8,128)} %copy-done.23) | copy-start | bytes 1572868
  1236.3 63.9 %copy-start.96 = (f32[1,1024]{1,0:T(1,128)S(1)}, f32[1,1024]{1,0:T(1,128)}, u32[]{:S(2)}) copy-start(f32[1,1024]{1,0:T(1,128)} %copy-done.94) | copy-start | bytes 12292
  1236.3 63.9 %copy-start.139 = (f32[128]{0:T(128)S(1)}, f32[128]{0:T(128)}, u32[]{:S(2)}) copy-start(f32[128]{0:T(128)} %copy-done.137) | copy-start | bytes 1540
  1236.3 63.9 %copy-start.148 = (f32[128]{0:T(128)S(1)}, f32[128]{0:T(128)}, u32[]{:S(2)}) copy-start(f32[128]{0:T(128)} %copy-done.147) | copy-start | bytes 1540
  (118 other events, 704.5 us)
Sparse Core Ops, SparseCore 0:
  11.7 30.5 all-gather.12
  106.8 53.9 all-reduce.4
  328.7 25.8 all-gather.14
  412.1 50.4 all-reduce.6
  787.1 24.6 all-gather.16
  824.8 7.7 reduce-scatter.10
  835.4 8.8 reduce-scatter.12
  847.7 29.0 reduce-scatter.14
  1045.8 24.6 all-gather.18
  1083.6 7.7 reduce-scatter.16
  1094.1 8.8 reduce-scatter.18
  1107.1 29.0 reduce-scatter.20
  1140.3 71.3 reduce-scatter.28
  1215.0 71.6 reduce-scatter.26
  1290.1 116.1 reduce-scatter.24
  1409.7 116.1 reduce-scatter.22
  1531.9 126.5 all-reduce.8
where the time goes:
time: 1680 us; the launch traced here: 1670 us
  waiting for transfers between devices  781 us (46%)
  blocking collectives  380 us (23%)
  matrix products  187 us (11%)
  local copies, waits for them, and re-layouts  144 us (9%)
  other arithmetic  113 us (7%)
  starting transfers between devices  45.8 us (3%)
  between operations  16.8 us (1%)
    reduce_scatter x2, waiting for transfers between devices, per_device(): lax.psum_scatter(grad_in_w.astype(jnp.bfloat16), ('dp', 'head'), scatter_...  219 us
    psum x1, waiting for transfers between devices, per_device(): lax.psum((jnp.stack(gain_a_list), jnp.stack(gain_m_list), jnp.stack(route...  126 us
    all_to_all x2, blocking collectives, per_device(): lax.all_to_all(send, 'expert', split_axis=0, concat_axis=0, tiled=True)  111 us
    all_to_all x2, blocking collectives, per_device(): lax.all_to_all(send_grad, 'expert', split_axis=0, concat_axis=0, tiled=True)  109 us
    all_to_all x2, waiting for transfers between devices, per_device(): lax.all_to_all(dinput_rows, 'expert', split_axis=0, concat_axis=0, tiled=...  99.2 us
    psum x2, waiting for transfers between devices, per_device(): lax.psum(jnp.dot(heads_flat, weight_o, preferred_element_type=jnp.float32...  91.3 us
    all_to_all x2, waiting for transfers between devices, per_device(): lax.all_to_all(expert_y, 'expert', split_axis=0, concat_axis=0, tiled=True)  82.1 us
    all_to_all x4, waiting for transfers between devices, sum_at_owner(): lax.all_to_all(pieces, axis, split_axis=0, concat_axis=0, tiled=True)  67.6 us
  transfers between devices with their start and end apart: 25, of which 20 were waited for; matrix products, arithmetic and copies ran while one was open for 9% of the time, Pallas kernels for 0%

commit v1 on v0

--- a/solution.py
+++ b/solution.py
@@ -1,7 +1,13 @@
+import functools
+
 import jax
 import jax.numpy as jnp
 from jax import lax
+from jax.experimental import pallas as pl
+from jax.experimental.pallas import tpu as pltpu
 from jax.sharding import PartitionSpec as P
+
+MESH = pl.DeviceIdType.MESH
 
 HEAD_DIM = 64
 BIDI = 256
@@ -93,7 +99,7 @@
     )
 
 
-def per_device(
+def per_device_rows(
     inputs,
     cotangent,
     segment_starts,
@@ -442,7 +448,628 @@
     )
 
 
+class Gather:
+    def __init__(self, axis):
+        self.axis = axis
+
+    def out(self, x, sizes):
+        return (sizes[self.axis],) + x.shape
+
+    def axes(self):
+        return (self.axis,)
+
+    def sems(self, sizes):
+        return sizes[self.axis] - 1, 1
+
+    def start(self, x, o, send, recv, local, sizes):
+        n, me = sizes[self.axis], lax.axis_index(self.axis)
+        self.copies = []
+        for k in range(1, n):
+            self.copies.append(
+                pltpu.make_async_remote_copy(
+                    src_ref=x,
+                    dst_ref=o.at[me],
+                    send_sem=send.at[k - 1],
+                    recv_sem=recv.at[k - 1],
+                    device_id={self.axis: lax.rem(me + k, n)},
+                    device_id_type=MESH,
+                )
+            )
+        for copy in self.copies:
+            copy.start()
+        self.own = pltpu.make_async_copy(x, o.at[me], local.at[0])
+        self.own.start()
+
+    def relay(self):
+        pass
+
+    def finish(self):
+        self.own.wait()
+        for copy in self.copies:
+            copy.wait()
+
+
+class Exchange(Gather):
+    def out(self, x, sizes):
+        return x.shape
+
+    def start(self, x, o, send, recv, local, sizes):
+        n, me = sizes[self.axis], lax.axis_index(self.axis)
+        self.copies = []
+        for k in range(1, n):
+            to = lax.rem(me + k, n)
+            self.copies.append(
+                pltpu.make_async_remote_copy(
+                    src_ref=x.at[to],
+                    dst_ref=o.at[me],
+                    send_sem=send.at[k - 1],
+                    recv_sem=recv.at[k - 1],
+                    device_id={self.axis: to},
+                    device_id_type=MESH,
+                )
+            )
+        for copy in self.copies:
+            copy.start()
+        self.own = pltpu.make_async_copy(x.at[me], o.at[me], local.at[0])
+        self.own.start()
+
+
+class Spread:
+    def __init__(self, shape=None, source=None, place=None):
+        self.shape = shape
+        self.source = source or (lambda x, d: x)
+        self.place = place or (lambda o, d, z: o.at[d, z])
+
+    def out(self, x, sizes):
+        return self.shape or (sizes["dp"], sizes["expert"]) + x.shape
+
+    def axes(self):
+        return ("expert", "dp")
+
+    def sems(self, sizes):
+        return 2 * sizes["expert"] - 1, 1
+
+    def start(self, x, o, send, recv, local, sizes):
+        n, z, d = sizes["expert"], lax.axis_index("expert"), lax.axis_index("dp")
+        mine, other = self.source(x, d), 1 - d
+        self.copies, self.onward = [], []
+        for k in range(1, n):
+            self.copies.append(
+                pltpu.make_async_remote_copy(
+                    src_ref=mine,
+                    dst_ref=self.place(o, d, z),
+                    send_sem=send.at[k - 1],
+                    recv_sem=recv.at[k - 1],
+                    device_id={"expert": lax.rem(z + k, n)},
+                    device_id_type=MESH,
+                )
+            )
+        for k in range(n):
+            origin = lax.rem(z - k + n, n)
+            self.onward.append(
+                pltpu.make_async_remote_copy(
+                    src_ref=mine if k == 0 else self.place(o, d, origin),
+                    dst_ref=self.place(o, d, origin),
+                    send_sem=send.at[n - 1 + k],
+                    recv_sem=recv.at[n - 1 + k],
+                    device_id={"dp": other},
+                    device_id_type=MESH,
+                )
+            )
+        for copy in self.copies:
+            copy.start()
+        self.onward[0].start()
+        self.own = pltpu.make_async_copy(mine, self.place(o, d, z), local.at[0])
+        self.own.start()
+
+    def relay(self):
+        for k, copy in enumerate(self.copies):
+            copy.wait_recv()
+            self.onward[k + 1].start()
+
+    def finish(self):
+        self.own.wait()
+        for copy in self.copies:
+            copy.wait_send()
+        for copy in self.onward:
+            copy.wait()
+
+
+class Swap:
+    def out(self, x, sizes):
+        return x.shape[1:]
+
+    def axes(self):
+        return ("dp",)
+
+    def sems(self, sizes):
+        return 1, 0
+
+    def start(self, x, o, send, recv, local, sizes):
+        other = 1 - lax.axis_index("dp")
+        self.copy = pltpu.make_async_remote_copy(
+            src_ref=x.at[other],
+            dst_ref=o,
+            send_sem=send.at[0],
+            recv_sem=recv.at[0],
+            device_id={"dp": other},
+            device_id_type=MESH,
+        )
+        self.copy.start()
+
+    def relay(self):
+        pass
+
+    def finish(self):
+        self.copy.wait()
+
+
+def transfer_body(makers, sizes, *refs):
+    count = len(makers)
+    ins, outs, sems = refs[:count], refs[count : 2 * count], refs[2 * count :]
+    tasks = [make() for make in makers]
+    axes = []
+    for task in tasks:
+        axes += [axis for axis in task.axes() if axis not in axes]
+    barrier = pltpu.get_barrier_semaphore()
+    greeted = 0
+    for axis in axes:
+        n, me = sizes[axis], lax.axis_index(axis)
+        for k in range(1, n):
+            pl.semaphore_signal(
+                barrier, inc=1, device_id={axis: lax.rem(me + k, n)}, device_id_type=MESH
+            )
+            greeted += 1
+    pl.semaphore_wait(barrier, greeted)
+    for t, task in enumerate(tasks):
+        task.start(ins[t], outs[t], *sems[3 * t : 3 * t + 3], sizes)
+    for task in tasks:
+        task.relay()
+    for task in tasks:
+        task.finish()
+
+
+def transfer(name, number, makers, arrays):
+    sizes = {axis: lax.axis_size(axis) for axis in ("dp", "expert", "head")}
+    tasks = [make() for make in makers]
+    scratch = []
+    for task in tasks:
+        remote, local = task.sems(sizes)
+        scratch += [
+            pltpu.SemaphoreType.DMA((remote,)),
+            pltpu.SemaphoreType.DMA((remote,)),
+            pltpu.SemaphoreType.DMA((max(1, local),)),
+        ]
+    vmem = pl.BlockSpec(memory_space=pltpu.VMEM)
+    return pl.pallas_call(
+        functools.partial(transfer_body, makers, sizes),
+        out_shape=[
+            jax.ShapeDtypeStruct(task.out(x, sizes), x.dtype) for task, x in zip(tasks, arrays)
+        ],
+        in_specs=[vmem] * len(arrays),
+        out_specs=[vmem] * len(arrays),
+        scratch_shapes=scratch,
+        compiler_params=pltpu.CompilerParams(collective_id=number, has_side_effects=True),
+        name=name,
+    )(*arrays)
+
+
+def token_plan_fits(mesh):
+    return mesh.shape["dp"] == 2 and mesh.shape["expert"] <= 8
+
+
+def per_device_dense(
+    inputs,
+    cotangent,
+    segment_starts,
+    routes,
+    attention_gain,
+    mixture_gain,
+    query_weight,
+    key_weight,
+    value_weight,
+    output_weight,
+    router_weight,
+    expert_in,
+    expert_out,
+):
+    f32, bf16 = jnp.float32, jnp.bfloat16
+    rows, width = inputs.shape
+    cores, owners, heads_axis = (lax.axis_size(a) for a in ("dp", "expert", "head"))
+    half_len = rows * heads_axis
+    length = half_len * cores
+    head_dim = HEAD_DIM
+    q_width, kv_width = query_weight.shape[2], key_weight.shape[2]
+    q_heads, kv_heads = q_width // head_dim, kv_width // head_dim
+    share = q_heads // kv_heads
+    layers = query_weight.shape[0]
+    own_experts = expert_in.shape[1]
+    per_core = own_experts // cores
+    all_experts = own_experts * owners
+    hidden_width = expert_out.shape[2]
+    group = rows * cores * owners
+    capacity = -(-cores * owners * CAP // 16) * 16
+    factor = head_dim ** (-0.5)
+    core, owner, place = (lax.axis_index(a) for a in ("dp", "expert", "head"))
+    offset = core * half_len
+    positions = jnp.arange(length, dtype=jnp.int32)
+    own_positions = offset + jnp.arange(half_len, dtype=jnp.int32)
+    cos_own, sin_own = rope_tables(own_positions, head_dim)
+    mask = visible(own_positions, positions, segment_starts[0])
+    first_expert = owner * own_experts + core * per_core
+
+    def dot(left, right, dims):
+        return lax.dot_general(left, right, (dims, ((), ())), preferred_element_type=f32)
+
+    wide = q_width + 2 * kv_width
+    piece = width // owners
+    packed = jnp.concatenate([query_weight, key_weight, value_weight], axis=2)
+    out_rows = output_weight.shape[1]
+
+    def weight_tasks():
+        return [
+            lambda: Spread(
+                (owners, cores, piece // cores, wide),
+                lambda x, d: x.at[d],
+                lambda o, d, z: o.at[z, d],
+            ),
+            lambda: Spread(
+                (cores, out_rows // cores, width),
+                lambda x, d: x.at[d],
+                lambda o, d, z: o.at[d, :, pl.ds(pl.multiple_of(z * piece, piece), piece)],
+            ),
+        ]
+
+    def weight_pieces(layer):
+        return [
+            packed[layer].reshape(cores, piece // cores, wide),
+            output_weight[layer].reshape(cores, out_rows // cores, piece),
+        ]
+
+    def whole_weights(arrived):
+        return arrived[0].reshape(width, wide), arrived[1].reshape(out_rows, width)
+
+    lanes = -(-layers * all_experts // 128) * 128
+    expert_ids = jnp.arange(all_experts, dtype=jnp.int32)
+    named = jnp.any(routes[..., None] == expert_ids, axis=2).astype(bf16)
+    named = jnp.moveaxis(named, 0, 1).reshape(rows, layers * all_experts)
+    named = jnp.pad(named, ((0, 0), (0, lanes - layers * all_experts)))
+
+    def normed(values, gain):
+        scale = rms_scale(values)
+        return scale, (values * scale * gain).astype(bf16)
+
+    current = inputs.astype(f32)
+    scale_one, normed_one = normed(current, attention_gain[0])
+    gathered, named_all, *weights_now = transfer(
+        "enter",
+        1,
+        [lambda: Gather("head"), lambda: Spread()] + weight_tasks(),
+        [normed_one, named] + weight_pieces(0),
+    )
+    named_all = named_all.reshape(group, lanes)
+    earlier = (
+        jnp.arange(group, dtype=jnp.int32)[:, None] < jnp.arange(group, dtype=jnp.int32)[None, :]
+    ).astype(bf16)
+    rank = dot(named_all, earlier, ((0,), (0,)))
+    named_t = named_all.astype(f32).T
+    slots = jnp.arange(capacity, dtype=jnp.int32).astype(f32)
+
+    def routing(layer):
+        base = layer * all_experts
+        hits = named_t[base : base + all_experts] > 0
+        local_rank = lax.dynamic_slice_in_dim(
+            rank[base : base + all_experts], first_expert, per_core, 0
+        )
+        local_hit = lax.dynamic_slice_in_dim(
+            named_t[base : base + all_experts], first_expert, per_core, 0
+        )
+        slot = jnp.where(local_hit > 0, local_rank, -1.0)
+        chosen = (slot[:, None, :] == slots[None, :, None]).astype(bf16)
+        return hits, chosen
+
+    def local_part(weights):
+        return lax.dynamic_slice_in_dim(weights, core * per_core, per_core, 0)
+
+    def to_homes(name, partial):
+        blocks = partial.astype(bf16).reshape(cores, owners, rows, width)
+        (other,) = transfer(name + "_core", 2, [lambda: Swap()], [blocks])
+        mine = lax.dynamic_index_in_dim(blocks, core, 0, keepdims=False)
+        both = (mine.astype(f32) + other.astype(f32)).astype(bf16)
+        (parts,) = transfer(name + "_owner", 3, [lambda: Exchange("expert")], [both])
+        return parts.astype(f32).sum(axis=0)
+
+    def over_heads(blocks):
+        if heads_axis != 4:
+            return lax.psum_scatter(blocks, "head", scatter_dimension=0, tiled=True)[0]
+        square = blocks.reshape(2, 2, *blocks.shape[1:])
+        spot = {0: place // 2, 1: place % 2}
+        done = []
+        for half, order in zip(jnp.split(square, [per_core // 2], axis=2), ((1, 0), (0, 1))):
+            for step, dim in enumerate(order):
+                pairs = [(i, i ^ (2 - dim)) for i in range(4)]
+                at = dim if step == 0 else 0
+                away = lax.dynamic_index_in_dim(half, 1 - spot[dim], at, keepdims=False)
+                here = lax.dynamic_index_in_dim(half, spot[dim], at, keepdims=False)
+                came = lax.ppermute(away, "head", pairs)
+                half = (here.astype(f32) + came.astype(f32)).astype(bf16)
+            done.append(half)
+        return jnp.concatenate(done, axis=0)
+
+    saved = []
+    for layer in range(layers):
+        weight_qkv, weight_o = whole_weights(weights_now)
+        own_rows = gathered.reshape(half_len, width)
+        lin = dot(own_rows, weight_qkv, ((1,), (0,)))
+        queries = rotate(
+            lin[:, :q_width].reshape(half_len, q_heads, head_dim), cos_own, sin_own, 1.0
+        ).astype(bf16)
+        own_keys = rotate(
+            lin[:, q_width : q_width + kv_width].reshape(half_len, kv_heads, head_dim),
+            cos_own,
+            sin_own,
+            1.0,
+        ).astype(bf16)
+        own_kv = jnp.concatenate(
+            [own_keys.reshape(half_len, kv_width), lin[:, q_width + kv_width :].astype(bf16)],
+            axis=1,
+        )
+        (both_kv,) = transfer("keys", 4, [lambda: Gather("dp")], [own_kv])
+        both_kv = both_kv.reshape(length, 2 * kv_width)
+        keys = both_kv[:, :kv_width].reshape(length, kv_heads, head_dim)
+        values = both_kv[:, kv_width:].reshape(length, kv_heads, head_dim)
+        grouped = queries.reshape(half_len, kv_heads, share, head_dim)
+        scores = jnp.einsum("qcgd,kcd->cgqk", grouped, keys, preferred_element_type=f32) * factor
+        scores = jnp.where(mask[None, None], scores, NEG)
+        peak = jnp.max(scores, axis=-1, keepdims=True)
+        raised = jnp.exp(scores - peak)
+        total = jnp.sum(raised, axis=-1, keepdims=True)
+        probs = (raised / total).astype(bf16)
+        heads_flat = (
+            jnp.einsum("cgqk,kcd->qcgd", probs, values, preferred_element_type=f32)
+            .astype(bf16)
+            .reshape(half_len, q_width)
+        )
+        log_total = peak + jnp.log(total)
+        partial = dot(heads_flat, weight_o, ((1,), (0,))).astype(bf16)
+        tasks, operands = [lambda: Exchange("head")], [partial.reshape(heads_axis, rows, width)]
+        if layer + 1 < layers:
+            tasks, operands = tasks + weight_tasks(), operands + weight_pieces(layer + 1)
+        parts, *weights_next = transfer(f"attended_{layer}", 5 + layer, tasks, operands)
+        middle = current + parts.astype(f32).sum(axis=0)
+        scale_two, normed_two = normed(middle, mixture_gain[layer])
+        (tokens,) = transfer("tokens", 10, [lambda: Spread()], [normed_two])
+        tokens = tokens.reshape(group, width)
+        hits, chosen = routing(layer)
+        logits = dot(router_weight[layer], tokens, ((0,), (1,)))
+        logits = jnp.where(hits, logits, NEG)
+        lifted = jnp.where(hits, jnp.exp(logits - jnp.max(logits, axis=0, keepdims=True)), 0.0)
+        gates = lifted / jnp.sum(lifted, axis=0, keepdims=True)
+        own_gates = lax.dynamic_slice_in_dim(gates, first_expert, per_core, 0)
+        received = jnp.einsum("jst,td->jsd", chosen, tokens, preferred_element_type=f32).astype(
+            bf16
+        )
+        w_in, w_out = local_part(expert_in[layer]), local_part(expert_out[layer])
+        mixed = jnp.einsum("jsd,jdf->jsf", received, w_in, preferred_element_type=f32)
+        gate_part, up_part = mixed[..., :hidden_width], mixed[..., hidden_width:]
+        hidden = (jax.nn.silu(gate_part) * up_part).astype(bf16)
+        expert_y = jnp.einsum("jsf,jfd->jsd", hidden, w_out, preferred_element_type=f32).astype(
+            bf16
+        )
+        weighted = (chosen.astype(f32) * own_gates[:, None, :]).astype(bf16)
+        mixture = to_homes(
+            "mixture",
+            dot(
+                weighted.reshape(per_core * capacity, group),
+                expert_y.reshape(per_core * capacity, width),
+                ((0,), (0,)),
+            ),
+        )
+        saved.append(
+            (
+                current,
+                scale_one,
+                own_rows,
+                weight_qkv,
+                weight_o,
+                grouped,
+                keys,
+                values,
+                heads_flat,
+                log_total,
+                middle,
+                scale_two,
+                chosen,
+                own_gates,
+                received,
+                gate_part,
+                up_part,
+                hidden,
+                expert_y,
+                mixture,
+                w_in,
+                w_out,
+            )
+        )
+        current = middle + mixture
+        if layer + 1 < layers:
+            scale_one, normed_one = normed(current, attention_gain[layer + 1])
+            (gathered,) = transfer("rows", 11, [lambda: Gather("head")], [normed_one])
+            weights_now = weights_next
+    outputs = current.astype(bf16)
+
+    grad = cotangent.astype(f32)
+    gains_a, gains_m, routers = [None] * layers, [None] * layers, [None] * layers
+    qkv_grads, out_grads = [None] * layers, [None] * layers
+    in_grads, down_grads = [None] * layers, [None] * layers
+    for layer in reversed(range(layers)):
+        (
+            state_in,
+            scale_one,
+            own_rows,
+            weight_qkv,
+            weight_o,
+            grouped,
+            keys,
+            values,
+            heads_flat,
+            log_total,
+            middle,
+            scale_two,
+            chosen,
+            own_gates,
+            received,
+            gate_part,
+            up_part,
+            hidden,
+            expert_y,
+            mixture,
+            w_in,
+            w_out,
+        ) = saved[layer]
+        grad_low = grad.astype(bf16)
+        inner = jnp.sum(grad_low.astype(f32) * mixture, axis=1)[None, :]
+        grads, inners = transfer(
+            "grads", 12, [lambda: Spread(), lambda: Spread()], [grad_low, inner]
+        )
+        grads, inners = grads.reshape(group, width), inners.reshape(group)
+        chosen_f = chosen.astype(f32)
+        row_gates = jnp.sum(chosen_f * own_gates[:, None, :], axis=-1, keepdims=True)
+        row_inner = jnp.sum(chosen_f * inners[None, None, :], axis=-1, keepdims=True)
+        row_grads = jnp.einsum("jst,td->jsd", chosen, grads, preferred_element_type=f32)
+        row_dgates = jnp.sum(row_grads * expert_y.astype(f32), axis=-1, keepdims=True)
+        dy = (row_gates * row_grads).astype(bf16)
+        dz = row_gates * (row_dgates - row_inner)
+        dhidden = jnp.einsum("jsd,jfd->jsf", dy, w_out, preferred_element_type=f32)
+        sigma = jax.nn.sigmoid(gate_part)
+        dgate = dhidden * up_part * sigma * (1.0 + gate_part * (1.0 - sigma))
+        dup = dhidden * (gate_part * sigma)
+        dmixed = jnp.concatenate([dgate, dup], axis=-1).astype(bf16)
+        router_rows = lax.dynamic_slice_in_dim(
+            router_weight[layer].T, first_expert, per_core, 0
+        ).astype(f32)
+        drow = jnp.einsum("jsf,jdf->jsd", dmixed, w_in, preferred_element_type=f32)
+        drow = (drow + dz * router_rows[:, None, :]).astype(bf16)
+        routers[layer] = jnp.sum(received.astype(f32) * dz, axis=1)
+        dnormed_two = to_homes(
+            "dtokens",
+            dot(
+                chosen.reshape(per_core * capacity, group),
+                drow.reshape(per_core * capacity, width),
+                ((0,), (0,)),
+            ),
+        )
+        grad_in = jnp.einsum(
+            "jspha,jsf->hjpaf",
+            received.reshape(per_core, capacity, cores, heads_axis, -1),
+            dmixed,
+            preferred_element_type=f32,
+        ).astype(bf16)
+        grad_down = jnp.einsum(
+            "jspha,jsd->hjpad",
+            hidden.reshape(per_core, capacity, cores, heads_axis, -1),
+            dy,
+            preferred_element_type=f32,
+        ).astype(bf16)
+        in_grads[layer] = over_heads(grad_in)
+        down_grads[layer] = over_heads(grad_down)
+        dmiddle, gains_m[layer] = norm_back(middle, scale_two, mixture_gain[layer], dnormed_two)
+        dmiddle = grad + dmiddle
+        (full_dattn,) = transfer("dattn", 11, [lambda: Gather("head")], [dmiddle.astype(bf16)])
+        full_dattn = full_dattn.reshape(half_len, width)
+        grad_o = dot(heads_flat, full_dattn, ((0,), (0,))).astype(bf16)
+        dheads = dot(full_dattn, weight_o, ((1,), (1,))).astype(bf16)
+        dgrouped = dheads.reshape(half_len, kv_heads, share, head_dim)
+        scores = jnp.einsum("qcgd,kcd->cgqk", grouped, keys, preferred_element_type=f32) * factor
+        scores = jnp.where(mask[None, None], scores, NEG)
+        probs = jnp.exp(scores - log_total)
+        dprobs = jnp.einsum("qcgd,kcd->cgqk", dgrouped, values, preferred_element_type=f32)
+        delta = jnp.sum(probs * dprobs, axis=-1, keepdims=True)
+        dscores = (probs * (dprobs - delta)).astype(bf16)
+        dqueries = jnp.einsum("cgqk,kcd->qcgd", dscores, keys, preferred_element_type=f32) * factor
+        dkeys = jnp.einsum("cgqk,qcgd->kcd", dscores, grouped, preferred_element_type=f32) * factor
+        dvalues = jnp.einsum(
+            "cgqk,qcgd->kcd", probs.astype(bf16), dgrouped, preferred_element_type=f32
+        )
+        dkv = jnp.concatenate(
+            [dkeys.reshape(length, kv_width), dvalues.reshape(length, kv_width)], axis=1
+        ).reshape(cores, half_len, 2 * kv_width)
+        (dkv_other,) = transfer("dkeys", 13, [lambda: Swap()], [dkv.astype(bf16)])
+        dkv = lax.dynamic_index_in_dim(dkv, core, 0, keepdims=False) + dkv_other.astype(f32)
+        dq_lin = rotate(
+            dqueries.reshape(half_len, q_heads, head_dim), cos_own, sin_own, -1.0
+        ).reshape(half_len, q_width)
+        dk_lin = rotate(
+            dkv[:, :kv_width].reshape(half_len, kv_heads, head_dim), cos_own, sin_own, -1.0
+        ).reshape(half_len, kv_width)
+        dlin = jnp.concatenate([dq_lin, dk_lin, dkv[:, kv_width:]], axis=1).astype(bf16)
+        grad_qkv = dot(own_rows, dlin, ((0,), (0,))).astype(bf16)
+        part = dot(dlin, weight_qkv, ((1,), (1,))).astype(bf16)
+        grad_qkv = grad_qkv.reshape(cores, owners, -1, wide)
+        grad_o = jnp.moveaxis(grad_o.reshape(out_rows, cores, owners, -1), 0, 2)
+        parts, qkv_other, out_other = transfer(
+            "dlin",
+            14,
+            [lambda: Exchange("head"), lambda: Swap(), lambda: Swap()],
+            [part.reshape(heads_axis, rows, width), grad_qkv, grad_o],
+        )
+
+        def with_other(blocks, other):
+            mine = lax.dynamic_index_in_dim(blocks, core, 0, keepdims=False)
+            return (mine.astype(f32) + other.astype(f32)).astype(bf16)
+
+        qkv_parts, out_parts = transfer(
+            "weight_grads",
+            15,
+            [lambda: Exchange("expert"), lambda: Exchange("expert")],
+            [with_other(grad_qkv, qkv_other), with_other(grad_o, out_other)],
+        )
+        qkv_grads[layer] = qkv_parts.astype(f32).sum(axis=0)
+        out_grads[layer] = out_parts.astype(f32).sum(axis=0)
+        dnormed_one = parts.astype(f32).sum(axis=0)
+        dstate, gains_a[layer] = norm_back(
+            state_in, scale_one, attention_gain[layer], dnormed_one
+        )
+        grad = dmiddle + dstate
+
+    def own_slices(pieces):
+        other = lax.dynamic_index_in_dim(pieces, 1 - core, 1, keepdims=False)
+        mine = lax.dynamic_index_in_dim(pieces, core, 1, keepdims=False)
+        swapped = lax.ppermute(other, "dp", [(0, 1), (1, 0)])
+        both = jnp.stack([mine, swapped])
+        first = lax.dynamic_index_in_dim(both, core, 0, keepdims=False)
+        second = lax.dynamic_index_in_dim(both, 1 - core, 0, keepdims=False)
+        return jnp.concatenate([first, second], axis=0).astype(f32)
+
+    small = jnp.concatenate(routers + [jnp.stack(gains_a), jnp.stack(gains_m)], axis=0)
+    (small,) = transfer("small_head", 16, [lambda: Gather("head")], [small])
+    (small,) = transfer("small_group", 17, [lambda: Spread()], [small.sum(axis=0)])
+    from_experts = layers * per_core
+    router_grad = (
+        small[:, :, :from_experts]
+        .reshape(cores, owners, layers, per_core, width)
+        .transpose(2, 4, 1, 0, 3)
+        .reshape(layers, width, all_experts)
+    )
+    gains = small[:, :, from_experts:].sum(axis=(0, 1))
+    qkv_grad = jnp.stack(qkv_grads)
+    return (
+        outputs,
+        grad,
+        gains[:layers],
+        gains[layers:],
+        qkv_grad[..., :q_width],
+        qkv_grad[..., q_width : q_width + kv_width],
+        qkv_grad[..., q_width + kv_width :],
+        jnp.stack(out_grads),
+        router_grad,
+        jnp.stack([own_slices(p) for p in in_grads]),
+        jnp.stack([own_slices(p) for p in down_grads]),
+    )
+
+
 def solution(mesh):
+    plan = per_device_dense if token_plan_fits(mesh) else per_device_rows
     in_specs = (
         P(("dp", "expert", "head"), None),
         P(("dp", "expert", "head"), None),
@@ -472,5 +1099,5 @@
         P(None, "expert", ("dp", "head"), None),
     )
     return jax.shard_map(
-        per_device, mesh=mesh, in_specs=in_specs, out_specs=out_specs, check_vma=False
+        plan, mesh=mesh, in_specs=in_specs, out_specs=out_specs, check_vma=False
     )

time: 1680 us -> 1080 us (0.64)
  waiting for transfers between devices: 781 us -> 136 us
  Pallas kernels: 0 us -> 484 us
  blocking collectives: 380 us -> 0 us
  matrix products: 187 us -> 153 us
  starting transfers between devices: 45.8 us -> 16.7 us
    pallas_call x0 -> x28, Pallas kernels: none -> 484 us  [transfer(): pl.pallas_call(functools.partial(transfer_body, makers, sizes), out_shape...]
    reduce_scatter x10 -> x0, waiting for transfers between devices: 265 us -> none  [the longest x2 219 us: per_device(): lax.psum_scatter(grad_in_w.astype(jnp.bfloat16), ('dp', 'head'), scatter_...]
    all_to_all x8 -> x0, waiting for transfers between devices: 249 us -> none  [the longest x2 99.2 us: per_device(): lax.all_to_all(dinput_rows, 'expert', split_axis=0, concat_axis=0, tiled=...]
    all_to_all x4 -> x0, blocking collectives: 220 us -> none  [the longest x2 111 us: per_device(): lax.all_to_all(send, 'expert', split_axis=0, concat_axis=0, tiled=True)]
    psum x3 -> x0, waiting for transfers between devices: 218 us -> none  [the longest x1 126 us: per_device(): lax.psum((jnp.stack(gain_a_list), jnp.stack(gain_m_list), jnp.stack(route...]
    ppermute x0 -> x20, waiting for transfers between devices: none -> 136 us  [the longest x16 136 us: over_heads(): came = lax.ppermute(away, 'head', pairs)]
    all_gather x8 -> x0, blocking collectives: 121 us -> none  [the longest x2 33.3 us: per_device(): lax.all_gather(output_weight[layer], 'expert', axis=1, tiled=True)]
    all_gather x4 -> x0, waiting for transfers between devices: 49.4 us -> none  [the longest x2 49.4 us: per_device(): lax.all_gather(dmiddle.astype(jnp.bfloat16), 'head', axis=0, tiled=True)]
  transfers between devices with their start and end apart: 25 -> 20, of which waited for: 20 -> 6; matrix products, arithmetic and copies ran while one was open for 9% -> 16% of each run, Pallas kernels for 0% -> 12%
where the time goes in v1:
time: 1080 us; the launch traced here: 1070 us
  Pallas kernels  484 us (45%)
  matrix products  153 us (14%)
  local copies, waits for them, and re-layouts  151 us (14%)
  waiting for transfers between devices  136 us (13%)
  other arithmetic  128 us (12%)
  starting transfers between devices  16.7 us (2%)
    pallas_call x28, Pallas kernels, transfer(): pl.pallas_call(functools.partial(transfer_body, makers, sizes), out_shape...  484 us
    ppermute x16, waiting for transfers between devices, over_heads(): came = lax.ppermute(away, 'head', pairs)  136 us
    dot_general x19, matrix products, dot(): lax.dot_general(left, right, (dims, ((), ())), preferred_element_type=f32)  58.9 us
    slice x2, local copies, waits for them, and re-layouts, per_device_dense(): w_in, w_out = (local_part(expert_in[layer]), local_part(expert_out[layer]))  33.5 us
    unnamed x310, local copies, waits for them, and re-layouts  30.7 us
  transfers between devices with their start and end apart: 20, of which 6 were waited for; matrix products, arithmetic and copies ran while one was open for 16% of the time, Pallas kernels for 12%

profile of v1, /device:TPU:0, one launch (start us, length us, event | category | flops | bytes accessed | tf_op | source)
XLA Modules:
  0.0 1071.9 jit_solution(13794007013850266437)
XLA Ops:
  8.6 30.0 %enter.1 = (bf16[4,128,1024]{2,1,0:T(8,128)(2,1)}, bf16[2,4,128,128]{3,2,1,0:T(8,128)(2,1)}, bf16[4,2,128,512]{3,2,1,0:T(8,128)(2,1)}, bf16[2,128,1024]{2,1,0:T(8,128)(2,1)}) custom-call(bf16[128,1024]{1,0:T(8,128)(2,1)} %fusion.179.refs_0_, bf16[128,128]{1,0:T(8,128)(2,1)} %pad_convert_fusion.refs_1_, bf16[2,128,512]{2,1,0:T(8,128)(2,1)} %bitcast.601, ...), custom_call_target="tpu_custom_call" | custom-call | tf_op jit(solution)/shard_map/enter/pallas_call | solution.py:644
  45.8 3.3 keys.2
  62.4 24.3 %attended_0.1 = (bf16[4,128,1024]{2,1,0:T(8,128)(2,1)}, bf16[4,2,128,512]{3,2,1,0:T(8,128)(2,1)}, bf16[2,128,1024]{2,1,0:T(8,128)(2,1)}) custom-call(bf16[4,128,1024]{2,1,0:T(8,128)(2,1)} %bitcast.551, bf16[2,128,512]{2,1,0:T(8,128)(2,1)} %bitcast.602, bf16[2,128,256]{2,1,0:T(8,128)(2,1)} %bitcast.614), custom_call_target="tpu_custom_call" | custom-call | tf_op jit(solution)/shard_map/attended_0/pallas_call | solution.py:644
  89.3 25.7 %tokens.2 = bf16[2,4,128,1024]{3,2,1,0:T(8,128)(2,1)} custom-call(bf16[128,1024]{1,0:T(8,128)(2,1)} %multiply_convert_fusion.14.refs_0_), custom_call_target="tpu_custom_call" | custom-call | tf_op jit(solution)/shard_map/tokens/pallas_call | solution.py:644
  115.1 23.6 %fusion.256 = (bf16[1,8,1024,1024]{3,2,1,0:T(8,128)(2,1)}, bf16[1,8,1024,1024]{3,2,1,0:T(8,128)(2,1)}) fusion(bf16[2,8,1024,1024]{3,2,1,0:T(8,128)(2,1)} %param.24), kind=kLoop, calls=%fused_computation.478 | loop fusion | bytes 67108864 | tf_op jit(solution)/shard_map/slice | solution.py:852
  142.6 4.1 copy-done.2
  151.4 9.8 fusion.257
  164.5 4.3 bitcast_convert_fusion.3
  168.8 5.2 mixture_core.2
  174.1 2.9 fusion.116.refs_0_
  177.0 27.8 %mixture_owner.2 = bf16[4,128,1024]{2,1,0:T(8,128)(2,1)} custom-call(bf16[4,128,1024]{2,1,0:T(8,128)(2,1)} %fusion.116.refs_0_), custom_call_target="tpu_custom_call" | custom-call | tf_op jit(solution)/shard_map/mixture_owner/pallas_call | solution.py:644
  207.2 16.8 %rows.1 = bf16[4,128,1024]{2,1,0:T(8,128)(2,1)} custom-call(bf16[128,1024]{1,0:T(8,128)(2,1)} %multiply_convert_fusion.13.refs_0_), custom_call_target="tpu_custom_call" | custom-call | tf_op jit(solution)/shard_map/rows/pallas_call | solution.py:644
  233.9 3.3 keys.3
  252.2 17.1 %attended_1.1 = bf16[4,128,1024]{2,1,0:T(8,128)(2,1)} custom-call(bf16[4,128,1024]{2,1,0:T(8,128)(2,1)} %bitcast.552), custom_call_target="tpu_custom_call" | custom-call | tf_op jit(solution)/shard_map/attended_1/pallas_call | solution.py:644
  271.8 30.0 %tokens.3 = bf16[2,4,128,1024]{3,2,1,0:T(8,128)(2,1)} custom-call(bf16[128,1024]{1,0:T(8,128)(2,1)} %multiply_convert_fusion.12.refs_0_), custom_call_target="tpu_custom_call" | custom-call | tf_op jit(solution)/shard_map/tokens/pallas_call | solution.py:644
  301.8 4.3 fusion.121
  306.1 6.7 fusion.8
  318.3 4.3 bitcast_convert_fusion.2
  322.6 5.2 mixture_core.3
  327.8 2.9 fusion.115.refs_0_
  330.8 28.0 %mixture_owner.3 = bf16[4,128,1024]{2,1,0:T(8,128)(2,1)} custom-call(bf16[4,128,1024]{2,1,0:T(8,128)(2,1)} %fusion.115.refs_0_), custom_call_target="tpu_custom_call" | custom-call | tf_op jit(solution)/shard_map/mixture_owner/pallas_call | solution.py:644
  361.7 34.7 %grads.2 = (bf16[2,4,128,1024]{3,2,1,0:T(8,128)(2,1)}, f32[2,4,1,128]{3,2,1,0:T(1,128)}) custom-call(bf16[128,1024]{1,0:T(8,128)(2,1)} %refs_0_, f32[1,128]{1,0:T(1,128)} %bitcast.640), custom_call_target="tpu_custom_call" | custom-call | tf_op jit(solution)/shard_map/grads/pallas_call | solution.py:644
  396.4 5.1 multiply_reduce_fusion.3
  402.7 7.0 multiply_convert_fusion.5
  411.1 10.7 bitcast_convert_fusion.1
  421.8 5.3 dtokens_core.2
  427.1 2.9 fusion.114.refs_0_
  430.0 24.0 %dtokens_owner.2 = bf16[4,128,1024]{2,1,0:T(8,128)(2,1)} custom-call(bf16[4,128,1024]{2,1,0:T(8,128)(2,1)} %fusion.114.refs_0_), custom_call_target="tpu_custom_call" | custom-call | tf_op jit(solution)/shard_map/dtokens_owner/pallas_call | solution.py:644
  457.2 16.4 %dattn.2 = bf16[4,128,1024]{2,1,0:T(8,128)(2,1)} custom-call(bf16[128,1024]{1,0:T(8,128)(2,1)} %fusion.252.refs_0_), custom_call_target="tpu_custom_call" | custom-call | tf_op jit(solution)/shard_map/dattn/pallas_call | solution.py:644
  478.2 5.3 fusion.3
  502.7 3.3 dkeys.2
  521.1 3.2 convolution_convert_fusion.6
  530.1 17.2 %dlin.2 = (bf16[4,128,1024]{2,1,0:T(8,128)(2,1)}, bf16[4,128,512]{2,1,0:T(8,128)(2,1)}, bf16[4,256,128]{2,1,0:T(8,128)(2,1)}) custom-call(bf16[4,128,1024]{2,1,0:T(8,128)(2,1)} %bitcast.592, bf16[2,4,128,512]{3,2,1,0:T(8,128)(2,1)} %bitcast.559, bf16[2,4,256,128]{3,2,1,0:T(8,128)(2,1)} %bitcast.553), custom_call_target="tpu_custom_call" | custom-call | tf_op jit(solution)/shard_map/dlin/pallas_call | solution.py:644
  551.6 33.9 %grads.3 = (bf16[2,4,128,1024]{3,2,1,0:T(8,128)(2,1)}, f32[2,4,1,128]{3,2,1,0:T(1,128)}) custom-call(bf16[128,1024]{1,0:T(8,128)(2,1)} %get-tuple-element.68.refs_0_, f32[1,128]{1,0:T(1,128)} %bitcast.637), custom_call_target="tpu_custom_call" | custom-call | tf_op jit(solution)/shard_map/grads/pallas_call | solution.py:644
  585.6 5.0 multiply_reduce_fusion.2
  604.2 4.7 fusion.172
  616.1 6.3 multiply_convert_fusion.3
  625.2 6.9 convolution_convert_fusion.1
  638.9 5.3 reshape.757
  644.1 10.8 %bitcast_convert_fusion = bf16[1024,1024]{1,0:T(8,128)(2,1)} fusion(bf16[1,8,1024,1024]{3,2,1,0:T(8,128)(2,1)} %get-tuple-element.81, s32[]{:T(128)S(6)} %select_n.153, f32[4,1024]{1,0:T(4,128)S(1)} %copy-done.120, f32[4,272]{1,0:T(4,128)S(1)} %subtract_multiply_fusion, f32[4,1024]{1,0:T(4,128)S(1)} %copy-done.99, f32[272]{0:T(512)S(1)} %copy-done.116, ...), kind=kOutput, calls=%fused_computation.79 | convolution fusion | flops 4573364224 | bytes 12752196 | tf_op jit(solution)/shard_map/dot_general | solution.py:702
  655.0 5.2 dtokens_core.3
  660.2 2.9 fusion.113.refs_0_
  663.2 23.9 %dtokens_owner.3 = bf16[4,128,1024]{2,1,0:T(8,128)(2,1)} custom-call(bf16[4,128,1024]{2,1,0:T(8,128)(2,1)} %fusion.113.refs_0_), custom_call_target="tpu_custom_call" | custom-call | tf_op jit(solution)/shard_map/dtokens_owner/pallas_call | solution.py:644
  690.4 16.0 %dattn.3 = bf16[4,128,1024]{2,1,0:T(8,128)(2,1)} custom-call(bf16[128,1024]{1,0:T(8,128)(2,1)} %get-tuple-element.65.refs_0_), custom_call_target="tpu_custom_call" | custom-call | tf_op jit(solution)/shard_map/dattn/pallas_call | solution.py:644
  710.7 5.2 fusion
  715.9 4.8 fusion.145
  720.7 5.1 fusion.2
  737.7 3.3 dkeys.3
  745.5 3.1 convolution_convert_fusion.4
  755.7 4.8 convolution_convert_fusion
  760.5 3.7 fusion.259
  765.9 27.1 %weight_grads.3 = (bf16[4,128,512]{2,1,0:T(8,128)(2,1)}, bf16[4,256,128]{2,1,0:T(8,128)(2,1)}) custom-call(bf16[4,128,512]{2,1,0:T(8,128)(2,1)} %fusion.170.refs_0_, bf16[4,256,128]{2,1,0:T(8,128)(2,1)} %fusion.212.refs_1_), custom_call_target="tpu_custom_call" | custom-call | tf_op jit(solution)/shard_map/weight_grads/pallas_call | solution.py:644
  795.3 17.0 %dlin.3 = (bf16[4,128,1024]{2,1,0:T(8,128)(2,1)}, bf16[4,128,512]{2,1,0:T(8,128)(2,1)}, bf16[4,256,128]{2,1,0:T(8,128)(2,1)}) custom-call(bf16[4,128,1024]{2,1,0:T(8,128)(2,1)} %bitcast.591, bf16[2,4,128,512]{3,2,1,0:T(8,128)(2,1)} %bitcast.561, bf16[2,4,256,128]{3,2,1,0:T(8,128)(2,1)} %bitcast.554), custom_call_target="tpu_custom_call" | custom-call | tf_op jit(solution)/shard_map/dlin/pallas_call | solution.py:644
  816.2 21.2 %weight_grads.2 = (bf16[4,128,512]{2,1,0:T(8,128)(2,1)}, bf16[4,256,128]{2,1,0:T(8,128)(2,1)}) custom-call(bf16[4,128,512]{2,1,0:T(8,128)(2,1)} %fusion.171.refs_0_, bf16[4,256,128]{2,1,0:T(8,128)(2,1)} %fusion.213.refs_1_), custom_call_target="tpu_custom_call" | custom-call | tf_op jit(solution)/shard_map/weight_grads/pallas_call | solution.py:644
  846.4 7.6 small_head.1
  855.6 10.7 %small_group.1 = f32[2,4,12,1024]{3,2,1,0:T(8,128)} custom-call(f32[12,1024]{1,0:T(8,128)} %reduce_sum.414.refs_0_), custom_call_target="tpu_custom_call" | custom-call | tf_op jit(solution)/shard_map/small_group/pallas_call | solution.py:644
  868.6 4.7 constant_dynamic-slice_fusion.5
  874.1 3.2 copy.237
  893.5 48.5 %collective-permute-done.13 = bf16[2,2,64,1024]{3,2,1,0:T(8,128)(2,1)S(1)} collective-permute-done((bf16[2,2,64,1024]{3,2,1,0:T(8,128)(2,1)S(1)}, bf16[2,2,64,1024]{3,2,1,0:T(8,128)(2,1)S(1)}, u32[]{:S(2)}, u32[]{:S(2)}) %collective-permute-start.13) | collective-permute-done | bytes 524320 | tf_op jit(solution)/shard_map/ppermute | solution.py:794
  944.3 8.9 collective-permute-done.18
  955.6 44.1 %collective-permute-done.16 = bf16[2,2,64,1024]{3,2,1,0:T(8,128)(2,1)S(1)} collective-permute-done((bf16[2,2,64,1024]{3,2,1,0:T(8,128)(2,1)S(1)}, bf16[2,2,64,1024]{3,2,1,0:T(8,128)(2,1)S(1)}, u32[]{:S(2)}, u32[]{:S(2)}) %collective-permute-start.16) | collective-permute-done | bytes 524320 | tf_op jit(solution)/shard_map/ppermute | solution.py:794
  1011.7 16.5 %collective-permute-done.3 = bf16[2,2,128,1024]{2,3,1,0:T(8,128)(2,1)S(1)} collective-permute-done((bf16[2,2,128,1024]{2,3,1,0:T(8,128)(2,1)S(1)}, bf16[2,2,128,1024]{2,3,1,0:T(8,128)(2,1)S(1)}, u32[]{:S(2)}, u32[]{:S(2)}) %collective-permute-start.3) | collective-permute-done | bytes 1048608 | tf_op jit(solution)/shard_map/ppermute | solution.py:794
  1033.6 16.7 %collective-permute-done.8 = bf16[2,2,128,1024]{2,3,1,0:T(8,128)(2,1)} collective-permute-done((bf16[2,2,128,1024]{2,3,1,0:T(8,128)(2,1)}, bf16[2,2,128,1024]{2,3,1,0:T(8,128)(2,1)}, u32[]{:S(2)}, u32[]{:S(2)}) %collective-permute-start.8) | collective-permute-done | bytes 1048608 | tf_op jit(solution)/shard_map/ppermute | solution.py:794
  1068.0 3.7 maximum_convert_fusion
  (591 shorter events, 272.6 us)
Async XLA Ops:
  1.5 39.5 %copy-start.93 = (f32[1,1024]{1,0:T(1,128)}, f32[1,1024]{1,0:T(1,128)S(1)}, u32[]{:S(2)}) copy-start(f32[1,1024]{1,0:T(1,128)S(1)} %get-tuple-element.163) | copy-start | bytes 12292
  2.6 38.4 %copy-start.129 = (f32[128]{0:T(128)}, f32[128]{0:T(128)S(1)}, u32[]{:S(2)}) copy-start(f32[128]{0:T(128)S(1)} %add_rsqrt_fusion.3) | copy-start | bytes 1540
  43.4 120.1 %copy-start.112 = (f32[272]{0:T(512)}, f32[272]{0:T(512)S(1)}, u32[]{:S(2)}) copy-start(f32[272]{0:T(512)S(1)} %iota_convert_fusion) | copy-start | bytes 3268
  61.0 25.8 %copy-start.69 = (bf16[2,64,2,512]{3,1,2,0:T(8,128)(2,1)}, bf16[2,64,2,512]{3,1,2,0:T(8,128)(2,1)S(1)}, u32[]{:S(2)}) copy-start(bf16[2,64,2,512]{3,1,2,0:T(8,128)(2,1)S(1)} %fusion.153) | copy-start | bytes 786436
  62.4 26.0 %copy-start.124 = (f32[2,1024]{1,0:T(2,128)S(1)}, f32[2,1024]{1,0:T(2,128)}, u32[]{:S(2)}) copy-start(f32[2,1024]{1,0:T(2,128)} %param.18) | copy-start | bytes 24580
  88.2 26.8 %copy-start.90 = (f32[128,1024]{1,0:T(8,128)S(1)}, f32[128,1024]{1,0:T(8,128)}, u32[]{:S(2)}) copy-start(f32[128,1024]{1,0:T(8,128)} %fusion.58) | copy-start | bytes 1572868
  88.4 117.8 %copy-start.14 = (f32[128,1024]{1,0:T(8,128)}, f32[128,1024]{1,0:T(8,128)S(1)}, u32[]{:S(2)}) copy-start(f32[128,1024]{1,0:T(8,128)S(1)} %get-tuple-element.79) | copy-start | bytes 1572868
  88.4 26.6 %copy-start.125 = (f32[128]{0:T(128)}, f32[128]{0:T(128)S(1)}, u32[]{:S(2)}) copy-start(f32[128]{0:T(128)S(1)} %add_rsqrt_fusion.2) | copy-start | bytes 1540
  88.4 26.6 %copy-start.95 = (f32[1,1024]{1,0:T(1,128)}, f32[1,1024]{1,0:T(1,128)S(1)}, u32[]{:S(2)}) copy-start(f32[1,1024]{1,0:T(1,128)S(1)} %get-tuple-element.161) | copy-start | bytes 12292
  115.1 25.1 %copy-start.22 = (bf16[2,4,128,1024]{3,2,1,0:T(8,128)(2,1)S(1)}, bf16[2,4,128,1024]{3,2,1,0:T(8,128)(2,1)}, u32[]{:S(2)}) copy-start(bf16[2,4,128,1024]{3,2,1,0:T(8,128)(2,1)} %tokens.2) | copy-start | bytes 6291460
  140.1 23.4 %copy-start.98 = (f32[4,1024]{1,0:T(4,128)}, f32[4,1024]{1,0:T(4,128)S(1)}, u32[]{:S(2)}) copy-start(f32[4,1024]{1,0:T(4,128)S(1)} %get-tuple-element.182) | copy-start | bytes 49156
  206.4 19.9 %copy-start.127 = (f32[128]{0:T(128)}, f32[128]{0:T(128)S(1)}, u32[]{:S(2)}) copy-start(f32[128]{0:T(128)S(1)} %add_rsqrt_fusion.1) | copy-start | bytes 1540
  250.7 18.6 %copy-start.70 = (bf16[2,64,2,512]{3,1,2,0:T(8,128)(2,1)}, bf16[2,64,2,512]{3,1,2,0:T(8,128)(2,1)S(1)}, u32[]{:S(2)}) copy-start(bf16[2,64,2,512]{3,1,2,0:T(8,128)(2,1)S(1)} %fusion.152) | copy-start | bytes 786436
  270.8 31.0 %copy-start.100 = (f32[4,1024]{1,0:T(4,128)S(1)}, f32[4,1024]{1,0:T(4,128)}, u32[]{:S(2)}) copy-start(f32[4,1024]{1,0:T(4,128)} %get-tuple-element.183) | copy-start | bytes 49156
  270.8 31.0 %copy-start.113 = (f32[272]{0:T(512)S(1)}, f32[272]{0:T(512)}, u32[]{:S(2)}) copy-start(f32[272]{0:T(512)} %copy-done.112) | copy-start | bytes 3268
  271.0 35.1 %copy-start.121 = (f32[128]{0:T(128)}, f32[128]{0:T(128)S(1)}, u32[]{:S(2)}) copy-start(f32[128]{0:T(128)S(1)} %add_rsqrt_fusion) | copy-start | bytes 1540
  301.8 15.0 %slice-start.4 = ((s8[8388608]{0:T(1024)(128)(4,1)}), s8[4194304]{0:T(1024)(128)(4,1)S(1)}, s32[]{:S(2)}) async-start(s8[8388608]{0:T(1024)(128)(4,1)} %bitcast.517), calls=%async_computation.4 | async-start | bytes 8388608
  330.8 30.2 %copy-start.42 = (bf16[128,1024]{1,0:T(8,128)(2,1)S(1)}, bf16[128,1024]{1,0:T(8,128)(2,1)}, u32[]{:S(2)}) copy-start(bf16[128,1024]{1,0:T(8,128)(2,1)} %refs_0_) | copy-start | bytes 786436
  330.8 65.6 %copy-start.101 = (f32[4,1024]{1,0:T(4,128)S(1)}, f32[4,1024]{1,0:T(4,128)}, u32[]{:S(2)}) copy-start(f32[4,1024]{1,0:T(4,128)} %get-tuple-element.183) | copy-start | bytes 49156
  330.8 65.6 %copy-start.114 = (f32[272]{0:T(512)S(1)}, f32[272]{0:T(512)}, u32[]{:S(2)}) copy-start(f32[272]{0:T(512)} %copy-done.112) | copy-start | bytes 3268
  361.0 41.7 %slice-start.8 = ((s8[4456448]{0:T(1024)(128)(4,1)}), s8[262144]{0:T(1024)(128)(4,1)S(1)}, s32[]{:S(2)}) async-start(s8[4456448]{0:T(1024)(128)(4,1)} %bitcast.521), calls=%async_computation.8 | async-start | bytes 524288
  409.8 12.1 %copy-start.108 = (f32[4,272]{1,0:T(4,128)}, f32[4,272]{1,0:T(4,128)S(1)}, u32[]{:S(2)}) copy-start(f32[4,272]{1,0:T(4,128)S(1)} %subtract_multiply_fusion.1) | copy-start | bytes 13060
  430.0 25.5 %copy-start.122 = (f32[128]{0:T(128)S(1)}, f32[128]{0:T(128)}, u32[]{:S(2)}) copy-start(f32[128]{0:T(128)} %copy-done.121) | copy-start | bytes 1540
  457.2 20.9 %copy-start.107 = (f32[2,2,512]{2,1,0:T(2,128)S(1)}, f32[2,2,512]{2,1,0:T(2,128)}, u32[]{:S(2)}) copy-start(f32[2,2,512]{2,1,0:T(2,128)} %copy-done.106) | copy-start | bytes 24580
  530.1 18.8 %copy-start.128 = (f32[128]{0:T(128)S(1)}, f32[128]{0:T(128)}, u32[]{:S(2)}) copy-start(f32[128]{0:T(128)} %copy-done.127) | copy-start | bytes 1540
  549.7 35.9 %copy-start.99 = (f32[4,1024]{1,0:T(4,128)S(1)}, f32[4,1024]{1,0:T(4,128)}, u32[]{:S(2)}) copy-start(f32[4,1024]{1,0:T(4,128)} %copy-done.98) | copy-start | bytes 49156
  549.7 35.9 %copy-start.116 = (f32[272]{0:T(512)S(1)}, f32[272]{0:T(512)}, u32[]{:S(2)}) copy-start(f32[272]{0:T(512)} %copy-done.112) | copy-start | bytes 3268
  599.0 283.2 %collective-permute-start.12 = (bf16[2,2,2,64,1024]{4,3,0,2,1:T(8,128)(2,1)}, bf16[2,2,2,64,1024]{4,3,0,2,1:T(8,128)(2,1)}, u32[]{:S(2)}, u32[]{:S(2)}) collective-permute-start(bf16[2,2,2,64,1024]{4,3,0,2,1:T(8,128)(2,1)} %dynamic-slice_bitcast_fusion.3), channel_id=1, source_target_pairs={{0,2},{1,3},{2,0},{3,1},{4,6},{5,7},{6,4},{7,5},{8,10},{9,11},{10,... | collective-permute-start | bytes 3145736 | tf_op jit(solution)/shard_map/ppermute | solution.py:794
  603.5 281.1 %collective-permute-start.10 = (bf16[2,2,2,64,1024]{4,3,2,1,0:T(8,128)(2,1)}, bf16[2,2,2,64,1024]{4,3,2,1,0:T(8,128)(2,1)}, u32[]{:S(2)}, u32[]{:S(2)}) collective-permute-start(bf16[2,2,2,64,1024]{4,3,2,1,0:T(8,128)(2,1)} %bitcast.510), channel_id=1, source_target_pairs={{0,1},{1,0},{2,3},{3,2},{4,5},{5,4},{6,7},{7,6},{8,9},{9,8},{10,11... | collective-permute-start | bytes 3145736 | tf_op jit(solution)/shard_map/ppermute | solution.py:794
  611.4 276.4 %collective-permute-start.17 = (bf16[2,2,2,64,1024]{4,3,0,2,1:T(8,128)(2,1)}, bf16[2,2,2,64,1024]{4,3,0,2,1:T(8,128)(2,1)}, u32[]{:S(2)}, u32[]{:S(2)}) collective-permute-start(bf16[2,2,2,64,1024]{4,3,0,2,1:T(8,128)(2,1)} %dynamic-slice_bitcast_fusion.2), channel_id=1, source_target_pairs={{0,2},{1,3},{2,0},{3,1},{4,6},{5,7},{6,4},{7,5},{8,10},{9,11},{10,... | collective-permute-start | bytes 3145736 | tf_op jit(solution)/shard_map/ppermute | solution.py:794
  614.2 276.0 %collective-permute-start.15 = (bf16[2,2,2,64,1024]{4,3,2,1,0:T(8,128)(2,1)}, bf16[2,2,2,64,1024]{4,3,2,1,0:T(8,128)(2,1)}, u32[]{:S(2)}, u32[]{:S(2)}) collective-permute-start(bf16[2,2,2,64,1024]{4,3,2,1,0:T(8,128)(2,1)} %bitcast.509), channel_id=1, source_target_pairs={{0,1},{1,0},{2,3},{3,2},{4,5},{5,4},{6,7},{7,6},{8,9},{9,8},{10,11... | collective-permute-start | bytes 3145736 | tf_op jit(solution)/shard_map/ppermute | solution.py:794
  638.0 361.9 %collective-permute-start.2 = (bf16[2,2,2,128,1024]{3,4,0,2,1:T(8,128)(2,1)}, bf16[2,2,2,128,1024]{3,4,0,2,1:T(8,128)(2,1)}, u32[]{:S(2)}, u32[]{:S(2)}) collective-permute-start(bf16[2,2,2,128,1024]{3,4,0,2,1:T(8,128)(2,1)} %dynamic-slice_bitcast_fusion.1), channel_id=1, source_target_pairs={{0,2},{1,3},{2,0},{3,1},{4,6},{5,7},{6,4},{7,5},{8,10},{9,11},{10,... | collective-permute-start | bytes 6291464 | tf_op jit(solution)/shard_map/ppermute | solution.py:794
  644.1 10.8 %copy-start.110 = (f32[4,272]{1,0:T(4,128)}, f32[4,272]{1,0:T(4,128)S(1)}, u32[]{:S(2)}) copy-start(f32[4,272]{1,0:T(4,128)S(1)} %subtract_multiply_fusion) | copy-start | bytes 13060
  663.2 25.4 %copy-start.15 = (f32[128,1024]{1,0:T(8,128)S(1)}, f32[128,1024]{1,0:T(8,128)}, u32[]{:S(2)}) copy-start(f32[128,1024]{1,0:T(8,128)} %copy-done.14) | copy-start | bytes 1572868
  663.2 25.4 %copy-start.96 = (f32[1,1024]{1,0:T(1,128)S(1)}, f32[1,1024]{1,0:T(1,128)}, u32[]{:S(2)}) copy-start(f32[1,1024]{1,0:T(1,128)} %copy-done.95) | copy-start | bytes 12292
  663.2 25.4 %copy-start.126 = (f32[128]{0:T(128)S(1)}, f32[128]{0:T(128)}, u32[]{:S(2)}) copy-start(f32[128]{0:T(128)} %copy-done.125) | copy-start | bytes 1540
  663.2 26.2 %copy-start.62 = (f32[128,1024]{1,0:T(8,128)S(1)}, f32[128,1024]{1,0:T(8,128)}, u32[]{:S(2)}) copy-start(f32[128,1024]{1,0:T(8,128)} %get-tuple-element.69) | copy-start | bytes 1572868
  690.4 18.5 %copy-start.79 = (bf16[2,128,1024]{2,1,0:T(8,128)(2,1)S(1)}, bf16[2,128,1024]{2,1,0:T(8,128)(2,1)}, u32[]{:S(2)}) copy-start(bf16[2,128,1024]{2,1,0:T(8,128)(2,1)} %get-tuple-element.34) | copy-start | bytes 1572868
  690.4 20.2 %copy-start.103 = (f32[2,2,512]{2,1,0:T(2,128)S(1)}, f32[2,2,512]{2,1,0:T(2,128)}, u32[]{:S(2)}) copy-start(f32[2,2,512]{2,1,0:T(2,128)} %copy-done.102) | copy-start | bytes 24580
  690.4 20.2 %copy-start.105 = (f32[2,2,512]{2,1,0:T(2,128)S(1)}, f32[2,2,512]{2,1,0:T(2,128)}, u32[]{:S(2)}) copy-start(f32[2,2,512]{2,1,0:T(2,128)} %copy-done.104) | copy-start | bytes 24580
  690.4 20.3 %copy-start.66 = (bf16[1024,128]{0,1:T(8,128)(2,1)S(1)}, bf16[1024,128]{0,1:T(8,128)(2,1)}, u32[]{:S(2)}) copy-start(bf16[1024,128]{0,1:T(8,128)(2,1)} %copy-done.65) | copy-start | bytes 786436
  764.2 29.8 %copy-start.58 = (bf16[256,1024]{1,0:T(8,128)(2,1)S(1)}, bf16[256,1024]{1,0:T(8,128)(2,1)}, u32[]{:S(2)}) copy-start(bf16[256,1024]{1,0:T(8,128)(2,1)} %convolution_convert_fusion.8) | copy-start | bytes 1572868
  795.3 17.0 %copy-start.51 = (bf16[256,2,4,128]{3,0,2,1:T(8,128)(2,1)S(1)}, bf16[256,2,4,128]{3,0,2,1:T(8,128)(2,1)}, u32[]{:S(2)}) copy-start(bf16[256,2,4,128]{3,0,2,1:T(8,128)(2,1)} %copy.166) | copy-start | bytes 1572868
  816.2 26.7 %copy-start.29 = (bf16[128,1024]{1,0:T(8,128)(2,1)S(1)}, bf16[128,1024]{1,0:T(8,128)(2,1)}, u32[]{:S(2)}) copy-start(bf16[128,1024]{1,0:T(8,128)(2,1)} %param.13) | copy-start | bytes 786436
  816.2 26.7 %copy-start.94 = (f32[1,1024]{1,0:T(1,128)S(1)}, f32[1,1024]{1,0:T(1,128)}, u32[]{:S(2)}) copy-start(f32[1,1024]{1,0:T(1,128)} %copy-done.93) | copy-start | bytes 12292
  882.2 120.7 %collective-permute-start = (bf16[2,2,2,128,1024]{3,4,2,1,0:T(8,128)(2,1)S(1)}, bf16[2,2,2,128,1024]{3,4,2,1,0:T(8,128)(2,1)S(1)}, u32[]{:S(2)}, u32[]{:S(2)}) collective-permute-start(bf16[2,2,2,128,1024]{3,4,2,1,0:T(8,128)(2,1)S(1)} %bitcast.566), channel_id=1, source_target_pairs={{0,1},{1,0},{2,3},{3,2},{4,5},{5,4},{6,7},{7,6},{8,9},{9,8},{10,11... | collective-permute-start | bytes 6291464 | tf_op jit(solution)/shard_map/ppermute | solution.py:794
  884.6 57.4 %collective-permute-start.13 = (bf16[2,2,64,1024]{3,2,1,0:T(8,128)(2,1)S(1)}, bf16[2,2,64,1024]{3,2,1,0:T(8,128)(2,1)S(1)}, u32[]{:S(2)}, u32[]{:S(2)}) collective-permute-start(bf16[2,2,64,1024]{3,2,1,0:T(8,128)(2,1)S(1)} %dynamic-slice_bitcast_fusion.10), channel_id=1, source_target_pairs={{0,1},{1,0},{2,3},{3,2},{4,5},{5,4},{6,7},{7,6},{8,9},{9,8},{10,11... | collective-permute-start | bytes 1572872 | tf_op jit(solution)/shard_map/ppermute | solution.py:794
  887.8 55.2 %collective-permute-start.11 = (bf16[2,2,64,1024]{3,2,1,0:T(8,128)(2,1)S(1)}, bf16[2,2,64,1024]{3,2,1,0:T(8,128)(2,1)S(1)}, u32[]{:S(2)}, u32[]{:S(2)}) collective-permute-start(bf16[2,2,64,1024]{3,2,1,0:T(8,128)(2,1)S(1)} %dynamic-slice_bitcast_fusion.11), channel_id=1, source_target_pairs={{0,2},{1,3},{2,0},{3,1},{4,6},{5,7},{6,4},{7,5},{8,10},{9,11},{10,... | collective-permute-start | bytes 1572872 | tf_op jit(solution)/shard_map/ppermute | solution.py:794
  890.3 62.9 %collective-permute-start.18 = (bf16[2,2,64,1024]{3,2,1,0:T(8,128)(2,1)S(1)}, bf16[2,2,64,1024]{3,2,1,0:T(8,128)(2,1)S(1)}, u32[]{:S(2)}, u32[]{:S(2)}) collective-permute-start(bf16[2,2,64,1024]{3,2,1,0:T(8,128)(2,1)S(1)} %dynamic-slice_bitcast_fusion.8), channel_id=1, source_target_pairs={{0,1},{1,0},{2,3},{3,2},{4,5},{5,4},{6,7},{7,6},{8,9},{9,8},{10,11... | collective-permute-start | bytes 1572872 | tf_op jit(solution)/shard_map/ppermute | solution.py:794
  891.6 51.4 %copy-start.59 = (bf16[2,1,2,2,128,1024]{4,5,3,2,0,1:T(8,128)(2,1)S(1)}, bf16[2,1,2,2,128,1024]{4,5,3,2,0,1:T(8,128)(2,1)}, u32[]{:S(2)}) copy-start(bf16[2,1,2,2,128,1024]{4,5,3,2,0,1:T(8,128)(2,1)} %copy.236) | copy-start | bytes 6291460
  942.0 62.9 %collective-permute-start.7 = (bf16[2,2,2,128,1024]{3,4,0,2,1:T(8,128)(2,1)S(1)}, bf16[2,2,2,128,1024]{3,4,0,2,1:T(8,128)(2,1)S(1)}, u32[]{:S(2)}, u32[]{:S(2)}) collective-permute-start(bf16[2,2,2,128,1024]{3,4,0,2,1:T(8,128)(2,1)S(1)} %dynamic-slice_bitcast_fusion), channel_id=1, source_target_pairs={{0,2},{1,3},{2,0},{3,1},{4,6},{5,7},{6,4},{7,5},{8,10},{9,11},{10,... | collective-permute-start | bytes 6291464 | tf_op jit(solution)/shard_map/ppermute | solution.py:794
  943.0 65.0 %collective-permute-start.5 = (bf16[2,2,2,128,1024]{3,4,2,1,0:T(8,128)(2,1)S(1)}, bf16[2,2,2,128,1024]{3,4,2,1,0:T(8,128)(2,1)S(1)}, u32[]{:S(2)}, u32[]{:S(2)}) collective-permute-start(bf16[2,2,2,128,1024]{3,4,2,1,0:T(8,128)(2,1)S(1)} %bitcast.565), channel_id=1, source_target_pairs={{0,1},{1,0},{2,3},{3,2},{4,5},{5,4},{6,7},{7,6},{8,9},{9,8},{10,11... | collective-permute-start | bytes 6291464 | tf_op jit(solution)/shard_map/ppermute | solution.py:794
  953.2 46.4 %collective-permute-start.16 = (bf16[2,2,64,1024]{3,2,1,0:T(8,128)(2,1)S(1)}, bf16[2,2,64,1024]{3,2,1,0:T(8,128)(2,1)S(1)}, u32[]{:S(2)}, u32[]{:S(2)}) collective-permute-start(bf16[2,2,64,1024]{3,2,1,0:T(8,128)(2,1)S(1)} %dynamic-slice_bitcast_fusion.9), channel_id=1, source_target_pairs={{0,2},{1,3},{2,0},{3,1},{4,6},{5,7},{6,4},{7,5},{8,10},{9,11},{10,... | collective-permute-start | bytes 1572872 | tf_op jit(solution)/shard_map/ppermute | solution.py:794
  954.2 45.7 %copy-start.11 = (bf16[2,2,2,2,128,1024]{4,5,1,0,3,2:T(8,128)(2,1)S(1)}, bf16[2,2,2,2,128,1024]{4,5,1,0,3,2:T(8,128)(2,1)}, u32[]{:S(2)}) copy-start(bf16[2,2,2,2,128,1024]{4,5,1,0,3,2:T(8,128)(2,1)} %copy-done.10) | copy-start | bytes 12582916
  999.6 58.0 %collective-permute-start.14 = (bf16[4,64,1024]{2,1,0:T(8,128)(2,1)}, bf16[4,64,1024]{2,1,0:T(8,128)(2,1)}, u32[]{:S(2)}, u32[]{:S(2)}) collective-permute-start(bf16[4,64,1024]{2,1,0:T(8,128)(2,1)} %get-tuple-element.114), channel_id=1, source_target_pairs={{0,16},{16,0},{1,17},{17,1},{2,18},{18,2},{3,19},{19,3},{4,20},{20... | collective-permute-start | bytes 1572872 | tf_op jit(solution)/shard_map/ppermute | solution.py:1038
  1002.1 26.1 %collective-permute-start.3 = (bf16[2,2,128,1024]{2,3,1,0:T(8,128)(2,1)S(1)}, bf16[2,2,128,1024]{2,3,1,0:T(8,128)(2,1)S(1)}, u32[]{:S(2)}, u32[]{:S(2)}) collective-permute-start(bf16[2,2,128,1024]{2,3,1,0:T(8,128)(2,1)S(1)} %dynamic-slice_bitcast_fusion.6), channel_id=1, source_target_pairs={{0,1},{1,0},{2,3},{3,2},{4,5},{5,4},{6,7},{7,6},{8,9},{9,8},{10,11... | collective-permute-start | bytes 3145736 | tf_op jit(solution)/shard_map/ppermute | solution.py:794
  1003.5 26.1 %collective-permute-start.1 = (bf16[2,2,128,1024]{2,3,1,0:T(8,128)(2,1)S(1)}, bf16[2,2,128,1024]{2,3,1,0:T(8,128)(2,1)S(1)}, u32[]{:S(2)}, u32[]{:S(2)}) collective-permute-start(bf16[2,2,128,1024]{2,3,1,0:T(8,128)(2,1)S(1)} %dynamic-slice_bitcast_fusion.7), channel_id=1, source_target_pairs={{0,2},{1,3},{2,0},{3,1},{4,6},{5,7},{6,4},{7,5},{8,10},{9,11},{10,... | collective-permute-start | bytes 3145736 | tf_op jit(solution)/shard_map/ppermute | solution.py:794
  1006.7 43.7 %collective-permute-start.8 = (bf16[2,2,128,1024]{2,3,1,0:T(8,128)(2,1)}, bf16[2,2,128,1024]{2,3,1,0:T(8,128)(2,1)}, u32[]{:S(2)}, u32[]{:S(2)}) collective-permute-start(bf16[2,2,128,1024]{2,3,1,0:T(8,128)(2,1)} %dynamic-slice_bitcast_fusion.4), channel_id=1, source_target_pairs={{0,1},{1,0},{2,3},{3,2},{4,5},{5,4},{6,7},{7,6},{8,9},{9,8},{10,11... | collective-permute-start | bytes 3145736 | tf_op jit(solution)/shard_map/ppermute | solution.py:794
  1008.6 19.9 %copy-start.19 = (bf16[2,2,2,128,1024]{3,4,2,1,0:T(8,128)(2,1)}, bf16[2,2,2,128,1024]{3,4,2,1,0:T(8,128)(2,1)S(1)}, u32[]{:S(2)}) copy-start(bf16[2,2,2,128,1024]{3,4,2,1,0:T(8,128)(2,1)S(1)} %fusion.45) | copy-start | bytes 6291460
  1009.7 42.1 %collective-permute-start.6 = (bf16[2,2,128,1024]{2,3,1,0:T(8,128)(2,1)}, bf16[2,2,128,1024]{2,3,1,0:T(8,128)(2,1)}, u32[]{:S(2)}, u32[]{:S(2)}) collective-permute-start(bf16[2,2,128,1024]{2,3,1,0:T(8,128)(2,1)} %dynamic-slice_bitcast_fusion.5), channel_id=1, source_target_pairs={{0,2},{1,3},{2,0},{3,1},{4,6},{5,7},{6,4},{7,5},{8,10},{9,11},{10,... | collective-permute-start | bytes 3145736 | tf_op jit(solution)/shard_map/ppermute | solution.py:794
  1028.2 30.9 %collective-permute-start.19 = (bf16[4,64,1024]{2,1,0:T(8,128)(2,1)}, bf16[4,64,1024]{2,1,0:T(8,128)(2,1)}, u32[]{:S(2)}, u32[]{:S(2)}) collective-permute-start(bf16[4,64,1024]{2,1,0:T(8,128)(2,1)} %get-tuple-element.118), channel_id=1, source_target_pairs={{0,16},{16,0},{1,17},{17,1},{2,18},{18,2},{3,19},{19,3},{4,20},{20... | collective-permute-start | bytes 1572872 | tf_op jit(solution)/shard_map/ppermute | solution.py:1038
  1033.6 18.2 %copy-start.20 = (bf16[2,2,2,128,1024]{3,4,2,1,0:T(8,128)(2,1)S(1)}, bf16[2,2,2,128,1024]{3,4,2,1,0:T(8,128)(2,1)}, u32[]{:S(2)}) copy-start(bf16[2,2,2,128,1024]{3,4,2,1,0:T(8,128)(2,1)} %copy-done.19) | copy-start | bytes 6291460
  1033.6 30.4 %collective-permute-start.4 = (bf16[4,128,1024]{2,1,0:T(8,128)(2,1)}, bf16[4,128,1024]{2,1,0:T(8,128)(2,1)}, u32[]{:S(2)}, u32[]{:S(2)}) collective-permute-start(bf16[4,128,1024]{2,1,0:T(8,128)(2,1)} %bitcast.589), channel_id=1, source_target_pairs={{0,16},{16,0},{1,17},{17,1},{2,18},{18,2},{3,19},{19,3},{4,20},{20... | collective-permute-start | bytes 3145736 | tf_op jit(solution)/shard_map/ppermute | solution.py:1038
  1054.9 11.1 %collective-permute-start.9 = (bf16[4,128,1024]{2,1,0:T(8,128)(2,1)}, bf16[4,128,1024]{2,1,0:T(8,128)(2,1)}, u32[]{:S(2)}, u32[]{:S(2)}) collective-permute-start(bf16[4,128,1024]{2,1,0:T(8,128)(2,1)} %bitcast.590), channel_id=1, source_target_pairs={{0,16},{16,0},{1,17},{17,1},{2,18},{18,2},{3,19},{19,3},{4,20},{20... | collective-permute-start | bytes 3145736 | tf_op jit(solution)/shard_map/ppermute | solution.py:1038
  (108 other events, 433.5 us)
